TPU v7x, 256 devices: a whole 4x4x8 slice. The times are simulated.
256 devices in a mesh: dp: 128 (over y, z, x), mp: 2 (over core).
Axes of the slice: x: 4, y: 4, z: 8, core: 2. Of those that a mesh axis runs over, the one named last changes fastest.
Arguments:
- hidden_state: bfloat16 [256, 19, 19, 256], P('dp'), may hold values from -6 to 6
- actions: int32 [256, 2], P('dp'), may hold values from 0 to 361
- value_target: int32 [256, 2], P('dp'), may hold values from 0 to 600
- reward_target: int32 [256, 2], P('dp'), may hold values from 0 to 600
- kernel_first: float32 [3, 3, 256, 256], P(None, None, 'dp', 'mp'), may hold values from -6 to 6
- kernel_second: float32 [3, 3, 256, 256], P(None, None, 'dp', 'mp'), may hold values from -6 to 6
- head_weight: float32 [2, 256, 601], P('mp', 'dp'), may hold values from -6 to 6
- action_embed: float32 [2, 256], P('mp', 'dp'), may hold values from -6 to 6
- first_mean: float32 [3, 3, 256, 256], P(None, None, 'dp', 'mp'), may hold values from -0.00061035156 to 0.00061035156
- first_square: float32 [3, 3, 256, 256], P(None, None, 'dp', 'mp'), may hold values from 1e-09 to 1e-06
- second_mean: float32 [3, 3, 256, 256], P(None, None, 'dp', 'mp'), may hold values from -0.00061035156 to 0.00061035156
- second_square: float32 [3, 3, 256, 256], P(None, None, 'dp', 'mp'), may hold values from 1e-09 to 1e-06
- head_mean: float32 [2, 256, 601], P('mp', 'dp'), may hold values from -0.0029296875 to 0.0029296875
- head_square: float32 [2, 256, 601], P('mp', 'dp'), may hold values from 1e-08 to 1e-06
- embed_mean: float32 [2, 256], P('mp', 'dp'), may hold values from -0.0017089844 to 0.0017089844
- embed_square: float32 [2, 256], P('mp', 'dp'), may hold values from 1e-09 to 1e-06
Outputs:
- kernel_first_new: float32 [3, 3, 256, 256], P(None, None, 'dp', 'mp')
- kernel_second_new: float32 [3, 3, 256, 256], P(None, None, 'dp', 'mp')
- head_weight_new: float32 [2, 256, 601], P('mp', 'dp')
- action_embed_new: float32 [2, 256], P('mp', 'dp')
- first_mean_new: float32 [3, 3, 256, 256], P(None, None, 'dp', 'mp')
- first_square_new: float32 [3, 3, 256, 256], P(None, None, 'dp', 'mp')
- second_mean_new: float32 [3, 3, 256, 256], P(None, None, 'dp', 'mp')
- second_square_new: float32 [3, 3, 256, 256], P(None, None, 'dp', 'mp')
- head_mean_new: float32 [2, 256, 601], P('mp', 'dp')
- head_square_new: float32 [2, 256, 601], P('mp', 'dp')
- embed_mean_new: float32 [2, 256], P('mp', 'dp')
- embed_square_new: float32 [2, 256], P('mp', 'dp')
- first_grad: float32 [3, 3, 256, 256], P(None, None, 'dp', 'mp')
- second_grad: float32 [3, 3, 256, 256], P(None, None, 'dp', 'mp')
- head_grad: float32 [2, 256, 601], P('mp', 'dp')
- embed_grad: float32 [2, 256], P('mp', 'dp')
Inputs may be any that keep to these rules, and one draw needn't show every extreme that they name: `actions`: the value 361 stands for a pass.
All inputs are finite; a program needn't handle non-finite values.
Results may differ from a plain program's by a relative error of at most 0.02.
Values may be sent and summed in bfloat16 or wider, within the bound.
A program may use at most 64 MiB of HBM per device.

v0:
```python
import functools

import jax
import jax.numpy as jnp
from jax import lax
from jax.experimental import pallas as pl
from jax.experimental.pallas import tpu as pltpu
from jax.sharding import Mesh
from jax.sharding import PartitionSpec as P

MESH = pl.DeviceIdType.MESH
CHANNELS = 256
DP = ("dp_0", "dp_1", "dp_2")
SIDE = 19
CELLS = 361
BUCKETS = 601
PITCH = 32
ROWS = SIDE * PITCH
TALL = 640
DEPTH = 704
ITEMS = 24
SCALE = (9.0 * CHANNELS) ** (-0.5)

head_scale = 4.0
soft_cap = 15.0
eps_norm = 1e-05
beta_one = 0.9
beta_two = 0.999
step_size = 0.1
eps_adam = 1e-08

F32 = jnp.float32
BF16 = jnp.bfloat16


def seats():
    return (
        lax.axis_index("dp_0"),
        lax.axis_index("dp_1"),
        lax.axis_index("dp_2"),
        lax.axis_index("mp"),
    )


def greet_all(y, z, x, c):
    barrier = pltpu.get_barrier_semaphore()
    for step in range(1, 8):
        pl.semaphore_signal(
            barrier, inc=1, device_id={"dp_1": lax.rem(z + step, 8)}, device_id_type=MESH
        )
    for step in range(1, 4):
        for name, here in (("dp_0", y), ("dp_2", x)):
            pl.semaphore_signal(
                barrier, inc=1, device_id={name: lax.rem(here + step, 4)}, device_id_type=MESH
            )
    pl.semaphore_signal(barrier, inc=1, device_id={"mp": 1 - c}, device_id_type=MESH)
    return barrier


def remote(src, dst, send, recv, peer):
    return pltpu.make_async_remote_copy(
        src_ref=src, dst_ref=dst, send_sem=send, recv_sem=recv, device_id=peer, device_id_type=MESH
    )


HALVES = (("dp_2", "dp_0"), ("dp_0", "dp_2"))
ORDER = (1, 3, 2)


def gather_kernel(
    first, second, head, embed, out, rows, stage, wide, z_send, z_recv, p_send, p_recv, q_send, q_recv,
    m_send, m_recv,
):
    y, z, x, c = seats()
    here = {"dp_0": y, "dp_2": x}
    barrier = greet_all(y, z, x, c)

    for tap in range(9):
        rows[2 * tap : 2 * tap + 2, :] = first[tap // 3, tap % 3]
        rows[18 + 2 * tap : 20 + 2 * tap, :] = second[tap // 3, tap % 3]
    rows[36:48, :] = jnp.zeros((12, 128), F32)
    for block in range(5):
        width = min(128, BUCKETS - 128 * block)
        rows[36 + 2 * block : 38 + 2 * block, 0:width] = head[0, :, 128 * block : 128 * block + width]
    for r in range(2):
        rows[46 + r : 47 + r, :] = jnp.broadcast_to(embed[:, r : r + 1], (1, 128))
    stage[z] = rows[...].astype(BF16)
    pl.semaphore_wait(barrier, 14)

    started = []
    for step in range(1, 8):
        copy = remote(
            stage.at[z], stage.at[z], z_send.at[step], z_recv.at[z], {"dp_1": lax.rem(z + step, 8)}
        )
        copy.start()
        started.append(copy)
    for step in range(1, 8):
        peer = lax.rem(z + step, 8)
        remote(stage.at[peer], stage.at[peer], z_send.at[0], z_recv.at[peer], {"dp_1": peer}).wait_recv()
    for piece in range(8):
        wide[56 * piece : 56 * piece + 48, :] = stage[piece].astype(F32)
    for item in range(ITEMS):
        low = wide[pl.ds(2 * item, 8, stride=56), :]
        high = wide[pl.ds(2 * item + 1, 8, stride=56), :]
        out[c, item, y, x] = jnp.concatenate([low, high], axis=0).astype(BF16)

    def part(half, near, far):
        items = pl.ds(12 * half, 12)
        if half == 0:
            return out.at[c, items, far, near]
        return out.at[c, items, near, far]

    def slab(half, far):
        items = pl.ds(12 * half, 12)
        if half == 0:
            return out.at[c, items, far]
        return out.at[c, items, :, far]

    for step in ORDER:
        for half, (near, far) in enumerate(HALVES):
            ref = part(half, here[near], here[far])
            copy = remote(
                ref, ref, p_send.at[half, step], p_recv.at[half, here[near]],
                {near: lax.rem(here[near] + step, 4)},
            )
            copy.start()
            started.append(copy)
    partner = {"mp": 1 - c}
    for half, (near, far) in enumerate(HALVES):
        for step in ORDER:
            peer = lax.rem(here[near] + step, 4)
            ref = part(half, peer, here[far])
            remote(ref, ref, p_send.at[half, 0], p_recv.at[half, peer], {near: peer}).wait_recv()
        ref = slab(half, here[far])
        for step in ORDER:
            copy = remote(
                ref, ref, q_send.at[half, step], q_recv.at[half, here[far]],
                {far: lax.rem(here[far] + step, 4)},
            )
            copy.start()
            started.append(copy)
        copy = remote(ref, ref, m_send.at[half, 0], m_recv.at[half, here[far], c], partner)
        copy.start()
        started.append(copy)
    for step in ORDER:
        for half, (near, far) in enumerate(HALVES):
            peer = lax.rem(here[far] + step, 4)
            ref = slab(half, peer)
            remote(ref, ref, q_send.at[half, 0], q_recv.at[half, peer], {far: peer}).wait_recv()
            copy = remote(ref, ref, m_send.at[half, step], m_recv.at[half, peer, c], partner)
            copy.start()
            started.append(copy)
    for half in range(2):
        for spot in range(4):
            items = pl.ds(12 * half, 12)
            ref = out.at[1 - c, items, spot] if half == 0 else out.at[1 - c, items, :, spot]
            remote(ref, ref, m_send.at[half, 0], m_recv.at[half, spot, 1 - c], partner).wait_recv()
    for copy in started:
        copy.wait_send()


def gather(first, second, head, embed):
    vmem = pl.BlockSpec(memory_space=pltpu.VMEM)
    dma = pltpu.SemaphoreType.DMA
    return pl.pallas_call(
        gather_kernel,
        out_shape=jax.ShapeDtypeStruct((2, ITEMS, 4, 4, 16, 128), BF16),
        in_specs=[vmem] * 4,
        out_specs=vmem,
        scratch_shapes=[
            pltpu.VMEM((48, 128), F32),
            pltpu.VMEM((8, 48, 128), BF16),
            pltpu.VMEM((448, 128), F32),
            dma((8,)),
            dma((8,)),
            dma((2, 4)),
            dma((2, 4)),
            dma((2, 4)),
            dma((2, 4)),
            dma((2, 4)),
            dma((2, 4, 2)),
        ],
        compiler_params=pltpu.CompilerParams(
            collective_id=0, has_side_effects=True, vmem_limit_bytes=16 << 20
        ),
        name="gather",
    )(first, second, head, embed)


def scatter_kernel(
    g, out, inbox, sums, a_in, b_in, a_sum, b_sum, a_last, b_last, flat, letters, m_send, m_recv, p_send, p_recv,
    q_send, q_recv, z_send, z_recv,
):
    y, z, x, c = seats()
    here = {"dp_0": y, "dp_2": x}
    barrier = greet_all(y, z, x, c)
    pl.semaphore_wait(barrier, 14)
    started = []

    def launch(copy):
        copy.start()
        started.append(copy)

    partner = {"mp": 1 - c}
    for half in range(2):
        items = pl.ds(12 * half, 12)
        launch(remote(g.at[1 - c, items], inbox.at[items], m_send.at[half], m_recv.at[half], partner))
    arrivals, folded, last = (a_in, b_in), (a_sum, b_sum), (a_last, b_last)
    for half, (near, far) in enumerate(HALVES):
        items = pl.ds(12 * half, 12)
        remote(g.at[1 - c, items], inbox.at[items], m_send.at[half], m_recv.at[half], partner).wait_recv()

        def join(item, carry):
            total = g[c, item].astype(F32) + inbox[item].astype(F32)
            sums[item] = total.astype(BF16)
            return carry

        lax.fori_loop(12 * half, 12 * half + 12, join, 0)
        for step in ORDER:
            peer = lax.rem(here[near] + step, 4)
            ref = sums.at[items, :, peer] if half == 0 else sums.at[items, peer]
            launch(
                remote(
                    ref, arrivals[half].at[here[near]], p_send.at[half, step], p_recv.at[half, here[near]],
                    {near: peer},
                )
            )
    for half, (near, far) in enumerate(HALVES):
        peers = [lax.rem(here[near] + step, 4) for step in (1, 2, 3)]
        for peer in peers:
            ref = arrivals[half].at[peer]
            remote(ref, ref, p_send.at[half, 0], p_recv.at[half, peer], {near: peer}).wait_recv()

        def fold(item, carry):
            own = sums[item, :, x] if half == 0 else sums[12 + item, y]
            total = own.astype(F32)
            for peer in peers:
                total = total + arrivals[half][peer, item].astype(F32)
            folded[half][item] = total.astype(BF16)
            return carry

        lax.fori_loop(0, 12, fold, 0)
        for step in ORDER:
            peer = lax.rem(here[far] + step, 4)
            launch(
                remote(
                    folded[half].at[:, peer], last[half].at[here[far]], q_send.at[half, step],
                    q_recv.at[half, here[far]], {far: peer},
                )
            )
    for half, (near, far) in enumerate(HALVES):
        peers = [lax.rem(here[far] + step, 4) for step in (1, 2, 3)]
        for peer in peers:
            ref = last[half].at[peer]
            remote(ref, ref, q_send.at[half, 0], q_recv.at[half, peer], {far: peer}).wait_recv()

        def settle(item, carry):
            total = folded[half][item, here[far]].astype(F32)
            for peer in peers:
                total = total + last[half][peer, item].astype(F32)
            flat[pl.ds(pl.multiple_of((12 * half + item) * 16, 16), 16), :] = total
            return carry

        lax.fori_loop(0, 12, settle, 0)
    for spot in range(8):
        letters[spot] = flat[pl.ds(spot, 48, stride=8), :].astype(BF16)
    for step in range(1, 8):
        peer = lax.rem(z + step, 8)
        launch(remote(letters.at[peer], out.at[z], z_send.at[step], z_recv.at[z], {"dp_1": peer}))
    out[z] = letters[z]
    for step in range(1, 8):
        peer = lax.rem(z + step, 8)
        remote(letters.at[peer], out.at[peer], z_send.at[0], z_recv.at[peer], {"dp_1": peer}).wait_recv()
    for copy in started:
        copy.wait_send()


def scatter(grads):
    vmem = pl.BlockSpec(memory_space=pltpu.VMEM)
    dma = pltpu.SemaphoreType.DMA
    return pl.pallas_call(
        scatter_kernel,
        out_shape=jax.ShapeDtypeStruct((8, 48, 128), BF16),
        in_specs=[vmem],
        out_specs=vmem,
        scratch_shapes=[
            pltpu.VMEM((ITEMS, 4, 4, 16, 128), BF16),
            pltpu.VMEM((ITEMS, 4, 4, 16, 128), BF16),
            pltpu.VMEM((4, 12, 4, 16, 128), BF16),
            pltpu.VMEM((4, 12, 4, 16, 128), BF16),
            pltpu.VMEM((12, 4, 16, 128), BF16),
            pltpu.VMEM((12, 4, 16, 128), BF16),
            pltpu.VMEM((4, 12, 16, 128), BF16),
            pltpu.VMEM((4, 12, 16, 128), BF16),
            pltpu.VMEM((384, 128), F32),
            pltpu.VMEM((8, 48, 128), BF16),
            dma((2,)),
            dma((2,)),
            dma((2, 4)),
            dma((2, 4)),
            dma((2, 4)),
            dma((2, 4)),
            dma((8,)),
            dma((8,)),
        ],
        compiler_params=pltpu.CompilerParams(
            collective_id=1, has_side_effects=True, vmem_limit_bytes=24 << 20
        ),
        name="scatter",
    )(grads)


NN = (((1,), (0,)), ((), ()))
NT = (((1,), (1,)), ((), ()))
TN = (((0,), (0,)), ((), ()))


def dot(a, b, dims=NN):
    return lax.dot_general(a, b, dims, preferred_element_type=F32)


def compute_kernel(
    moves, values, rewards, hidden_in, w, out, xs, hs, bs, zs, xt, bt, state, mixed, pre, summed, saved
):
    c = lax.axis_index("mp")
    row = lax.broadcasted_iota(jnp.int32, (ROWS, CHANNELS), 0)
    valid = lax.rem(row, PITCH) < SIDE

    def first(tap):
        return jnp.concatenate([w[0, tap], w[1, tap]], axis=1)

    def second(tap):
        return jnp.concatenate([w[0, 9 + tap], w[1, 9 + tap]], axis=1)

    def head(h):
        return jnp.concatenate([w[h, 18 + k] for k in range(5)], axis=1)

    def conv(field, kernel, flip):
        taps = [8 - t if flip else t for t in range(9)]
        lhs = jnp.concatenate(
            [field[t % 3, PITCH * (t // 3) : PITCH * (t // 3) + ROWS] for t in range(9)], axis=1
        )
        return lhs, [kernel(t) for t in taps]

    def conv_plain(field, kernel, flip):
        lhs, parts = conv(field, kernel, flip)
        return dot(lhs, jnp.concatenate(parts, axis=0))

    def conv_swapped(field, kernel, flip):
        lhs, parts = conv(field, kernel, flip)
        return dot(lhs, jnp.concatenate(parts, axis=1), NT)

    def spread(value, dest):
        dest[1, PITCH : PITCH + ROWS] = value.astype(BF16)
        dest[0, PITCH : PITCH + ROWS] = pltpu.roll(value, 1, 0).astype(BF16)
        dest[2, PITCH : PITCH + ROWS] = pltpu.roll(value, ROWS - 1, 0).astype(BF16)

    def turned(value):
        tall = jnp.concatenate([value, jnp.zeros((TALL - ROWS, CHANNELS), F32)], axis=0)
        return tall.T.astype(BF16)

    def total(value):
        return jnp.sum(jnp.sum(value, axis=0, keepdims=True), axis=1, keepdims=True)

    for field in (xs, hs, bs, zs):
        for k in range(2):
            for b in range(3):
                field[k, b, 0:PITCH] = jnp.zeros((PITCH, CHANNELS), BF16)
                field[k, b, PITCH + ROWS : DEPTH] = jnp.zeros((DEPTH - PITCH - ROWS, CHANNELS), BF16)

    lane = lax.broadcasted_iota(jnp.int32, (CHANNELS, CHANNELS), 1)
    natural = 64 * (lane // 64) + 8 * (lane % 8) + 2 * ((lane // 16) % 4) + (lane // 8) % 2
    source = lax.broadcasted_iota(jnp.int32, (CHANNELS, CHANNELS), 0)
    permute = (source == natural).astype(BF16)
    state[...] = jnp.zeros((ROWS, CHANNELS), F32)
    for line in range(SIDE):
        state[PITCH * line : PITCH * line + SIDE, :] = hidden_in[c, line].astype(F32)
    state[...] = dot(state[...].astype(BF16), permute)

    ones = jnp.ones((16, 128), BF16)
    pick = lax.broadcasted_iota(jnp.int32, (16, 128), 1) == 0
    pick = jnp.where(pick, ones, jnp.zeros_like(ones))
    embed = [dot(pick, w[e, 23], NT)[0:1, :] for e in range(2)]

    bucket = lax.broadcasted_iota(jnp.int32, (16, 640), 1)
    kept = []
    pooled_rows = jnp.zeros((16, CHANNELS), F32)
    grad_rows = [jnp.zeros((16, 640), F32) for _ in range(2)]
    for k in range(2):
        move = moves[c, k]
        spot = PITCH * lax.div(move, SIDE) + lax.rem(move, SIDE)
        passed = move == CELLS
        added = jnp.where(row == spot, embed[0], 0.0) + jnp.where(passed, 1.0, 0.0) * embed[1]
        now = jnp.where(valid, state[...] + added, 0.0)
        mixed[...] = now
        spread(now, xs.at[k])
        xt[:, TALL * k : TALL * k + TALL] = turned(now)
        value = SCALE * conv_plain(xs.at[k], first, False)
        pre[k] = value
        spread(jnp.where(valid, value * jax.nn.sigmoid(value), 0.0), hs.at[k])
        branch = conv_swapped(hs.at[k], second, False)
        value = jnp.where(valid, mixed[...] + SCALE * branch, 0.0)
        summed[k] = value
        factor = lax.rsqrt(total(value * value) / (CELLS * CHANNELS) + eps_norm)
        value = value * factor
        state[...] = value
        pooled = (jnp.sum(value, axis=0, keepdims=True) / CELLS).astype(BF16)
        pooled = jnp.broadcast_to(pooled.astype(F32), (16, CHANNELS))
        own_row = lax.broadcasted_iota(jnp.int32, (16, CHANNELS), 0) == k
        pooled_rows = jnp.where(own_row, pooled, pooled_rows)
        pooled = pooled.astype(BF16)
        pooled_grad = jnp.zeros((16, CHANNELS), F32)
        for h, targets in enumerate((values, rewards)):
            raw = head_scale * dot(pooled, head(h))
            squashed = jnp.tanh(raw / soft_cap)
            raised = jnp.where(bucket < BUCKETS, jnp.exp(soft_cap * squashed), 0.0)
            chances = raised / jnp.sum(raised, axis=1, keepdims=True)
            picked = jnp.where(bucket == targets[c, k], 1.0, 0.0)
            logit = (chances - picked) * (1.0 - squashed * squashed) / 256.0
            logit = jnp.where(bucket < BUCKETS, logit, 0.0).astype(BF16)
            pooled_grad = pooled_grad + dot(logit, head(h), NT)
            logit = logit.astype(F32)
            own_row = lax.broadcasted_iota(jnp.int32, (16, 640), 0) == k
            grad_rows[h] = jnp.where(own_row, logit, grad_rows[h])
        kept.append((spot, passed, factor, head_scale * pooled_grad[0:1, :] / CELLS))

    for h in range(2):
        grad = head_scale * dot(pooled_rows.astype(BF16), grad_rows[h].astype(BF16), TN)
        for block in range(5):
            out[h, 18 + block] = grad[:, 128 * block : 128 * block + 128].astype(BF16)

    embed_grad = [jnp.zeros((1, CHANNELS), F32) for _ in range(2)]
    for k in (1, 0):
        spot, passed, factor, pooled_grad = kept[k]
        grad = pooled_grad if k == 1 else saved[...] + pooled_grad
        grad = jnp.where(valid, grad, 0.0)
        value = summed[k]
        slope = total(grad * value) / (CELLS * CHANNELS)
        summed_grad = factor * grad - factor * factor * factor * value * slope
        saved[...] = summed_grad
        spread(summed_grad, bs.at[k])
        bt[:, TALL * k : TALL * k + TALL] = turned(summed_grad)
        hidden_grad = SCALE * conv_plain(bs.at[k], second, True)
        value = pre[k]
        sig = jax.nn.sigmoid(value)
        inner = hidden_grad * (sig * (1.0 + value * (1.0 - sig)))
        spread(jnp.where(valid, inner, 0.0), zs.at[k])
        carry = saved[...] + SCALE * conv_swapped(zs.at[k], first, True)
        carry = jnp.where(valid, carry, 0.0)
        saved[...] = carry
        embed_grad[0] = embed_grad[0] + jnp.sum(jnp.where(row == spot, carry, 0.0), axis=0, keepdims=True)
        embed_grad[1] = embed_grad[1] + jnp.where(passed, 1.0, 0.0) * jnp.sum(carry, axis=0, keepdims=True)

    for e in range(2):
        rows = jnp.broadcast_to(embed_grad[e], (16, CHANNELS)).astype(BF16)
        top = lax.broadcasted_iota(jnp.int32, (16, 128), 0) == 0
        out[e, 23] = dot(rows, jnp.where(top, ones, jnp.zeros_like(ones)), TN).astype(BF16)

    def window(field, tap):
        start = PITCH * (tap // 3)
        return jnp.concatenate([field[k, tap % 3, start : start + TALL] for k in range(2)], axis=0)

    for tap in range(9):
        grad = SCALE * dot(bt[...], window(hs, tap))
        out[0, 9 + tap] = grad[:, 0:128].astype(BF16)
        out[1, 9 + tap] = grad[:, 128:256].astype(BF16)
    for tap in range(9):
        grad = SCALE * dot(xt[...], window(zs, 8 - tap))
        out[0, tap] = grad[:, 0:128].astype(BF16)
        out[1, tap] = grad[:, 128:256].astype(BF16)


def compute(moves, values, rewards, hidden_state, weights):
    vmem = pl.BlockSpec(memory_space=pltpu.VMEM)
    smem = pl.BlockSpec(memory_space=pltpu.SMEM)
    copies = pltpu.VMEM((2, 3, DEPTH, CHANNELS), BF16)
    field = pltpu.VMEM((ROWS, CHANNELS), F32)
    fields = pltpu.VMEM((2, ROWS, CHANNELS), F32)
    return pl.pallas_call(
        compute_kernel,
        out_shape=jax.ShapeDtypeStruct((2, ITEMS, CHANNELS, 128), BF16),
        in_specs=[smem, smem, smem, vmem, vmem],
        out_specs=vmem,
        scratch_shapes=[
            copies,
            copies,
            copies,
            copies,
            pltpu.VMEM((CHANNELS, 2 * TALL), BF16),
            pltpu.VMEM((CHANNELS, 2 * TALL), BF16),
            field,
            field,
            fields,
            fields,
            field,
        ],
        compiler_params=pltpu.CompilerParams(vmem_limit_bytes=56 << 20),
        name="compute",
    )(moves, values, rewards, hidden_state, weights)


def adam(param, grad, mean, square):
    mean_new = beta_one * mean + (1.0 - beta_one) * grad
    square_new = beta_two * square + (1.0 - beta_two) * grad * grad
    param_new = param - step_size * mean_new / (jnp.sqrt(square_new) + eps_adam)
    return param_new, mean_new, square_new, grad


def adam_kernel(parts, *refs):
    params, means, squares, outs = refs[0:4], refs[4:8], refs[8:12], refs[12:]
    new, mean_new, square_new, grads = outs[0:4], outs[4:8], outs[8:12], outs[12:16]
    total = parts[0].astype(F32)
    for piece in range(1, 8):
        total = total + parts[piece].astype(F32)
    for which in range(2):
        for tap in range(9):
            a, b, at = tap // 3, tap % 3, 18 * which + 2 * tap
            results = adam(
                params[which][a, b], total[at : at + 2], means[which][a, b], squares[which][a, b]
            )
            for ref, result in zip((new, mean_new, square_new, grads), results):
                ref[which][a, b] = result
    head = jnp.concatenate([total[36 + 2 * k : 38 + 2 * k] for k in range(5)], axis=1)[:, 0:BUCKETS]
    results = adam(params[2][0], head, means[2][0], squares[2][0])
    for ref, result in zip((new, mean_new, square_new, grads), results):
        ref[2][0] = result
    embed = jnp.concatenate([total[46:47, 0:1], total[47:48, 0:1]], axis=1)
    results = adam(params[3][...], embed, means[3][...], squares[3][...])
    for ref, result in zip((new, mean_new, square_new, grads), results):
        ref[3][...] = result


def updates(parts, params, means, squares):
    vmem = pl.BlockSpec(memory_space=pltpu.VMEM)
    shapes = [jax.ShapeDtypeStruct(p.shape, F32) for p in params]
    return pl.pallas_call(
        adam_kernel,
        out_shape=shapes * 4,
        in_specs=[vmem] * 13,
        out_specs=[vmem] * 16,
        compiler_params=pltpu.CompilerParams(vmem_limit_bytes=8 << 20),
        name="adam",
    )(parts, *params, *means, *squares)


def local(
    hidden_state,
    actions,
    value_target,
    reward_target,
    kernel_first,
    kernel_second,
    head_weight,
    action_embed,
    first_mean,
    first_square,
    second_mean,
    second_square,
    head_mean,
    head_square,
    embed_mean,
    embed_square,
):
    params = (kernel_first, kernel_second, head_weight, action_embed)
    weights = gather(*params).reshape(2, ITEMS, CHANNELS, 128)
    grads = compute(actions, value_target, reward_target, hidden_state, weights)
    parts = scatter(grads.reshape(2, ITEMS, 4, 4, 16, 128))
    outs = updates(
        parts,
        params,
        (first_mean, second_mean, head_mean, embed_mean),
        (first_square, second_square, head_square, embed_square),
    )
    new, means, squares, sums = outs[0:4], outs[4:8], outs[8:12], outs[12:16]
    moments = [moment for pair in zip(means, squares) for moment in pair]
    return (*new, *moments, *sums)


def solution(mesh):
    torus = Mesh(mesh.devices.reshape(4, 8, 4, mesh.shape["mp"]), ("dp_0", "dp_1", "dp_2", "mp"))
    kernel = P(None, None, DP, "mp")
    head = P("mp", DP, None)
    embed = P("mp", DP)
    rows = P(DP, None)
    placed = (P(DP, None, None, None), rows, rows, rows, kernel, kernel, head, embed)
    moments = (kernel, kernel, kernel, kernel, head, head, embed, embed)
    return jax.shard_map(
        local,
        mesh=torus,
        in_specs=placed + moments,
        out_specs=(kernel, kernel, head, embed) + moments + (kernel, kernel, head, embed),
        check_vma=False,
    )
```

profile of v0, /device:TPU:2, one launch (start us, length us, event | category | flops | bytes accessed | tf_op | source)
XLA Modules:
  0.0 88.4 jit_solution(113721736698807912)
XLA Ops:
  0.6 1.8 %copy.32.hidden_in = bf16[2,19,19,256]{3,2,1,0:T(8,128)(2,1)} copy(bf16[2,19,19,256]{3,0,2,1:T(2,128)(2,1)} %param.16) | data formatting | bytes 739328 | tf_op args[0]
  2.5 0.7 copy-done.2
  3.2 0.7 copy-done.4
  3.9 0.7 copy-done.6
  4.6 0.7 copy-done.14
  5.2 28.7 %gather.1 = bf16[2,24,4,4,16,128]{5,4,3,2,1,0:T(8,128)(2,1)S(1)} custom-call(f32[3,3,2,128]{3,2,1,0:T(2,128)S(1)} %copy-done.2, f32[3,3,2,128]{3,2,1,0:T(2,128)S(1)} %copy-done.4, f32[1,2,601]{2,1,0:T(2,128)S(1)} %copy-done.6, f32[1,2]{1,0:T(1,128)S(1)} %copy-done.14), custom_call_target="tpu_custom_call" | custom-call | tf_op jit(solution)/shard_map/gather/pallas_call | solution.py:165
  33.9 0.0 copy-start.1
  33.9 1.6 %copy-done.1 = bf16[2,24,4,4,16,128]{5,4,3,2,1,0:T(8,128)(2,1)} copy-done((bf16[2,24,4,4,16,128]{5,4,3,2,1,0:T(8,128)(2,1)}, bf16[2,24,4,4,16,128]{5,4,3,2,1,0:T(8,128)(2,1)S(1)}, u32[]{:S(2)}) %copy-start.1) | copy-done | bytes 3145752
  35.5 20.8 %compute.1 = bf16[2,24,256,128]{3,2,1,0:T(8,128)(2,1)} custom-call(s32[2,2]{1,0:T(2,128)} %moves.1, s32[2,2]{1,0:T(2,128)} %values.1, s32[2,2]{1,0:T(2,128)} %rewards.1, bf16[2,19,19,256]{3,2,1,0:T(8,128)(2,1)} %copy.32.hidden_in, bf16[2,24,256,128]{3,2,1,0:T(8,128)(2,1)} %bitcast.3), custom_call_target="tpu_custom_call" | custom-call | tf_op jit(solution)/shard_map/compute/pallas_call | solution.py:479
  56.4 0.0 copy-start
  56.4 1.9 %copy-done = bf16[2,24,256,128]{3,2,1,0:T(8,128)(2,1)S(1)} copy-done((bf16[2,24,256,128]{3,2,1,0:T(8,128)(2,1)S(1)}, bf16[2,24,256,128]{3,2,1,0:T(8,128)(2,1)}, u32[]{:S(2)}) %copy-start) | copy-done | bytes 3145752
  58.3 0.0 copy-start.9
  58.3 0.0 copy-start.10
  58.3 0.0 copy-start.11
  58.3 0.0 copy-start.12
  58.3 0.0 copy-start.13
  58.4 29.2 %scatter.1.parts = bf16[8,48,128]{2,1,0:T(8,128)(2,1)S(1)} custom-call(bf16[2,24,4,4,16,128]{5,4,3,2,1,0:T(8,128)(2,1)S(1)} %bitcast.2), custom_call_target="tpu_custom_call" | custom-call | tf_op jit(solution)/shard_map/scatter/pallas_call | solution.py:281
  87.6 0.0 copy-done.15
  87.6 0.0 copy-done.16
  87.6 0.0 copy-done.17
  87.6 0.0 copy-done.3
  87.6 0.0 copy-done.5
  87.6 0.0 copy-done.7
  87.7 0.7 adam.1
  (17 shorter events, 0.0 us)
Async XLA Ops:
  2.5 0.7 copy-start.2
  3.2 0.7 copy-start.4
  3.9 0.7 copy-start.6
  4.6 0.7 copy-start.14
  33.9 1.6 %copy-start.1 = (bf16[2,24,4,4,16,128]{5,4,3,2,1,0:T(8,128)(2,1)}, bf16[2,24,4,4,16,128]{5,4,3,2,1,0:T(8,128)(2,1)S(1)}, u32[]{:S(2)}) copy-start(bf16[2,24,4,4,16,128]{5,4,3,2,1,0:T(8,128)(2,1)S(1)} %gather.1) | copy-start | bytes 9437188
  56.3 31.3 %copy-start.15 = (f32[1,2]{1,0:T(1,128)S(1)}, f32[1,2]{1,0:T(1,128)}, u32[]{:S(2)}) copy-start(f32[1,2]{1,0:T(1,128)} %refs_3_.1) | copy-start | bytes 28
  56.3 31.3 %copy-start.16 = (f32[1,2]{1,0:T(1,128)S(1)}, f32[1,2]{1,0:T(1,128)}, u32[]{:S(2)}) copy-start(f32[1,2]{1,0:T(1,128)} %refs_7_.1) | copy-start | bytes 28
  56.3 31.3 %copy-start.17 = (f32[1,2]{1,0:T(1,128)S(1)}, f32[1,2]{1,0:T(1,128)}, u32[]{:S(2)}) copy-start(f32[1,2]{1,0:T(1,128)} %refs_11_.1) | copy-start | bytes 28
  56.4 1.9 %copy-start = (bf16[2,24,256,128]{3,2,1,0:T(8,128)(2,1)S(1)}, bf16[2,24,256,128]{3,2,1,0:T(8,128)(2,1)}, u32[]{:S(2)}) copy-start(bf16[2,24,256,128]{3,2,1,0:T(8,128)(2,1)} %compute.1) | copy-start | bytes 9437188
  58.3 29.3 %copy-start.3 = (f32[3,3,2,128]{3,2,1,0:T(2,128)S(1)}, f32[3,3,2,128]{3,2,1,0:T(2,128)}, u32[]{:S(2)}) copy-start(f32[3,3,2,128]{3,2,1,0:T(2,128)} %refs_0_.1) | copy-start | bytes 27652
  58.3 29.4 %copy-start.5 = (f32[3,3,2,128]{3,2,1,0:T(2,128)S(1)}, f32[3,3,2,128]{3,2,1,0:T(2,128)}, u32[]{:S(2)}) copy-start(f32[3,3,2,128]{3,2,1,0:T(2,128)} %refs_1_.1) | copy-start | bytes 27652
  58.3 29.4 %copy-start.7 = (f32[1,2,601]{2,1,0:T(2,128)S(1)}, f32[1,2,601]{2,1,0:T(2,128)}, u32[]{:S(2)}) copy-start(f32[1,2,601]{2,1,0:T(2,128)} %refs_2_.1) | copy-start | bytes 14428
  58.3 29.4 %copy-start.8 = (f32[3,3,2,128]{3,2,1,0:T(2,128)S(1)}, f32[3,3,2,128]{3,2,1,0:T(2,128)}, u32[]{:S(2)}) copy-start(f32[3,3,2,128]{3,2,1,0:T(2,128)} %refs_4_.1) | copy-start | bytes 27652
  58.3 29.4 %copy-start.9 = (f32[3,3,2,128]{3,2,1,0:T(2,128)S(1)}, f32[3,3,2,128]{3,2,1,0:T(2,128)}, u32[]{:S(2)}) copy-start(f32[3,3,2,128]{3,2,1,0:T(2,128)} %refs_5_.1) | copy-start | bytes 27652
  58.3 29.4 %copy-start.10 = (f32[3,3,2,128]{3,2,1,0:T(2,128)S(1)}, f32[3,3,2,128]{3,2,1,0:T(2,128)}, u32[]{:S(2)}) copy-start(f32[3,3,2,128]{3,2,1,0:T(2,128)} %refs_8_.1) | copy-start | bytes 27652
  58.3 29.4 %copy-start.11 = (f32[3,3,2,128]{3,2,1,0:T(2,128)S(1)}, f32[3,3,2,128]{3,2,1,0:T(2,128)}, u32[]{:S(2)}) copy-start(f32[3,3,2,128]{3,2,1,0:T(2,128)} %refs_9_.1) | copy-start | bytes 27652
  58.3 29.4 %copy-start.12 = (f32[1,2,601]{2,1,0:T(2,128)S(1)}, f32[1,2,601]{2,1,0:T(2,128)}, u32[]{:S(2)}) copy-start(f32[1,2,601]{2,1,0:T(2,128)} %refs_6_.1) | copy-start | bytes 14428
  58.3 29.4 %copy-start.13 = (f32[1,2,601]{2,1,0:T(2,128)S(1)}, f32[1,2,601]{2,1,0:T(2,128)}, u32[]{:S(2)}) copy-start(f32[1,2,601]{2,1,0:T(2,128)} %refs_10_.1) | copy-start | bytes 14428
where the time goes:
time: 89.2 us; the launch traced here: 88.4 us
  Pallas kernels  79.4 us (89%)
  local copies, waits for them, and re-layouts  8.19 us (9%)
    pallas_call x1, Pallas kernels, scatter(): pl.pallas_call(scatter_kernel, out_shape=jax.ShapeDtypeStruct((8, 48, 128...  29.2 us
    pallas_call x1, Pallas kernels, gather(): pl.pallas_call(gather_kernel, out_shape=jax.ShapeDtypeStruct((2, ITEMS, 4...  28.7 us
    pallas_call x1, Pallas kernels, compute(): pl.pallas_call(compute_kernel, out_shape=jax.ShapeDtypeStruct((2, ITEMS,...  20.8 us
    unnamed x37, local copies, waits for them, and re-layouts  8.19 us

commit v1 on v0

v1 whole, which is shorter than its diff:
```python
import functools

import jax
import jax.numpy as jnp
from jax import lax
from jax.experimental import pallas as pl
from jax.experimental.pallas import tpu as pltpu
from jax.sharding import Mesh
from jax.sharding import PartitionSpec as P

MESH = pl.DeviceIdType.MESH
CHANNELS = 256
DP = ("dp_0", "dp_1", "dp_2")
SIDE = 19
CELLS = 361
BUCKETS = 601
PITCH = 32
ROWS = SIDE * PITCH
TALL = 640
DEPTH = 704
ITEMS = 24
HEAD, SECOND, FIRST, EMBED = 0, 5, 14, 23
CHUNKS = (((0, 2, 0), (2, 3, 0)), ((5, 5, 2), (10, 4, 3)), ((14, 5, 7), (19, 5, 7)))
HALVES = (("dp_2", "dp_0"), ("dp_0", "dp_2"))
ORDER = (1, 3, 2)
SCALE = (9.0 * CHANNELS) ** (-0.5)

head_scale = 4.0
soft_cap = 15.0
eps_norm = 1e-05
beta_one = 0.9
beta_two = 0.999
step_size = 0.1
eps_adam = 1e-08

F32 = jnp.float32
BF16 = jnp.bfloat16


def seats():
    return (
        lax.axis_index("dp_0"),
        lax.axis_index("dp_1"),
        lax.axis_index("dp_2"),
        lax.axis_index("mp"),
    )


def greet_all(y, z, x, c):
    barrier = pltpu.get_barrier_semaphore()
    for step in range(1, 8):
        pl.semaphore_signal(
            barrier, inc=1, device_id={"dp_1": lax.rem(z + step, 8)}, device_id_type=MESH
        )
    for step in range(1, 4):
        for name, here in (("dp_0", y), ("dp_2", x)):
            pl.semaphore_signal(
                barrier, inc=1, device_id={name: lax.rem(here + step, 4)}, device_id_type=MESH
            )
    pl.semaphore_signal(barrier, inc=1, device_id={"mp": 1 - c}, device_id_type=MESH)
    return barrier


def remote(src, dst, send, recv, peer):
    return pltpu.make_async_remote_copy(
        src_ref=src, dst_ref=dst, send_sem=send, recv_sem=recv, device_id=peer, device_id_type=MESH
    )


def arrived(ref, recv, send, peer):
    remote(ref, ref, send, recv, peer).wait_recv()


class Gather:
    def __init__(self, seat, w, stage, wide, sems, started):
        self.y, self.z, self.x, self.c = seat
        self.here = {"dp_0": self.y, "dp_2": self.x}
        self.w, self.stage, self.wide, self.started = w, stage, wide, started
        self.z_send, self.z_recv, self.p_send, self.p_recv = sems[0:4]
        self.q_send, self.q_recv, self.r_send, self.r_recv, self.m_send, self.m_recv = sems[4:10]
        self.partner = {"mp": 1 - self.c}

    def launch(self, copy):
        copy.start()
        self.started.append(copy)

    def tile(self, chunk, half, near, far):
        start, count, _ = CHUNKS[chunk][half]
        items = pl.ds(start, count)
        if half == 0:
            return self.w.at[self.c, items, far, near]
        return self.w.at[self.c, items, near, far]

    def slab(self, chunk, half, far, core, part=None):
        start, count, _ = CHUNKS[chunk][half]
        items = pl.ds(start, count)
        span = pl.ds(0, 4) if part is None else pl.ds(2 * part, 2)
        if half == 0:
            return self.w.at[core, items, far, span]
        return self.w.at[core, items, span, far]

    def along_z(self):
        z = self.z
        for step in range(1, 8):
            peer = {"dp_1": lax.rem(z + step, 8)}
            ref = self.stage.at[z]
            self.launch(remote(ref, ref, self.z_send.at[step], self.z_recv.at[z], peer))

    def near_sends(self):
        z = self.z
        for step in range(1, 8):
            peer = lax.rem(z + step, 8)
            arrived(self.stage.at[peer], self.z_recv.at[peer], self.z_send.at[0], {"dp_1": peer})
        for piece in range(8):
            self.wide[56 * piece : 56 * piece + 48, :] = self.stage[piece].astype(F32)
        for chunk in (2, 1, 0):
            for half, (near, far) in enumerate(HALVES):
                start, count, _ = CHUNKS[chunk][half]
                for item in range(start, start + count):
                    low = self.wide[pl.ds(2 * item, 8, stride=56), :]
                    high = self.wide[pl.ds(2 * item + 1, 8, stride=56), :]
                    block = jnp.concatenate([low, high], axis=0).astype(BF16)
                    self.w[self.c, item, self.y, self.x] = block
            for step in ORDER:
                for half, (near, far) in enumerate(HALVES):
                    at = self.here[near]
                    ref = self.tile(chunk, half, at, self.here[far])
                    self.launch(
                        remote(
                            ref, ref, self.p_send.at[chunk, half, step], self.p_recv.at[chunk, half, at],
                            {near: lax.rem(at + step, 4)},
                        )
                    )

    def to_partner(self, chunk, half, piece, ref):
        self.launch(
            remote(
                ref, ref, self.m_send.at[chunk, half, piece], self.m_recv.at[chunk, half, piece], self.partner
            )
        )

    def far_sends(self, chunk):
        for half, (near, far) in enumerate(HALVES):
            for step in ORDER:
                peer = lax.rem(self.here[near] + step, 4)
                ref = self.tile(chunk, half, peer, self.here[far])
                arrived(ref, self.p_recv.at[chunk, half, peer], self.p_send.at[chunk, half, 0], {near: peer})
            at = self.here[far]
            ref = self.slab(chunk, half, at, self.c)
            for way, step in enumerate((1, 3)):
                self.launch(
                    remote(
                        ref, ref, self.q_send.at[chunk, half, way], self.q_recv.at[chunk, half, way],
                        {far: lax.rem(at + step, 4)},
                    )
                )
            self.to_partner(chunk, half, 0, ref)

    def relays(self, chunk):
        for half, (near, far) in enumerate(HALVES):
            at = self.here[far]
            for way, (step, back) in enumerate(((1, 3), (3, 1))):
                peer = lax.rem(at + back, 4)
                ref = self.slab(chunk, half, peer, self.c)
                arrived(ref, self.q_recv.at[chunk, half, way], self.q_send.at[chunk, half, way], {far: peer})
                part = self.slab(chunk, half, peer, self.c, way)
                self.launch(
                    remote(
                        part, part, self.r_send.at[chunk, half, way], self.r_recv.at[chunk, half, way],
                        {far: lax.rem(at + step, 4)},
                    )
                )
                self.to_partner(chunk, half, 1 + way, ref)

    def finish(self, chunk):
        for half, (near, far) in enumerate(HALVES):
            peer = lax.rem(self.here[far] + 2, 4)
            for way in range(2):
                part = self.slab(chunk, half, peer, self.c, way)
                arrived(part, self.r_recv.at[chunk, half, way], self.r_send.at[chunk, half, way], {far: peer})
                self.to_partner(chunk, half, 3 + way, part)
        for half, (near, far) in enumerate(HALVES):
            at, other = self.here[far], 1 - self.c
            refs = [self.slab(chunk, half, lax.rem(at + step, 4), other) for step in (0, 3, 1)]
            refs += [self.slab(chunk, half, lax.rem(at + 2, 4), other, way) for way in range(2)]
            for piece, ref in enumerate(refs):
                sems = self.m_recv.at[chunk, half, piece], self.m_send.at[chunk, half, piece]
                arrived(ref, *sems, self.partner)


class Scatter:
    def __init__(self, seat, g, buffers, sems, started):
        self.y, self.z, self.x, self.c = seat
        self.here = {"dp_0": self.y, "dp_2": self.x}
        self.g, self.started = g, started
        self.inbox, self.sums, a_in, b_in, a_sum, b_sum, a_last, b_last, self.flat = buffers
        self.arrivals, self.folded, self.last = (a_in, b_in), (a_sum, b_sum), (a_last, b_last)
        self.m_send, self.m_recv, self.p_send, self.p_recv = sems[0:4]
        self.q_send, self.q_recv, self.z_send, self.z_recv = sems[4:8]
        self.partner = {"mp": 1 - self.c}

    def launch(self, copy):
        copy.start()
        self.started.append(copy)

    def across(self, chunk, half):
        start, count, _ = CHUNKS[chunk][half]
        items = pl.ds(start, count)
        return remote(
            self.g.at[1 - self.c, items], self.inbox.at[items], self.m_send.at[chunk, half],
            self.m_recv.at[chunk, half], self.partner,
        )

    def to_partner(self, chunk, half):
        self.launch(self.across(chunk, half))

    def near_sends(self, chunk, half):
        near, far = HALVES[half]
        start, count, at = CHUNKS[chunk][half]
        self.across(chunk, half).wait_recv()

        def join(item, carry):
            total = self.g[self.c, item].astype(F32) + self.inbox[item].astype(F32)
            self.sums[item] = total.astype(BF16)
            return carry

        lax.fori_loop(start, start + count, join, 0)
        items = pl.ds(start, count)
        for step in ORDER:
            peer = lax.rem(self.here[near] + step, 4)
            ref = self.sums.at[items, :, peer] if half == 0 else self.sums.at[items, peer]
            self.launch(
                remote(
                    ref, self.arrivals[half].at[self.here[near], pl.ds(at, count)],
                    self.p_send.at[chunk, half, step], self.p_recv.at[chunk, half, self.here[near]], {near: peer},
                )
            )

    def far_sends(self, chunk, half):
        near, far = HALVES[half]
        start, count, at = CHUNKS[chunk][half]
        peers = [lax.rem(self.here[near] + step, 4) for step in (1, 2, 3)]
        box, total_of = self.arrivals[half], self.folded[half]
        for peer in peers:
            ref = box.at[peer, pl.ds(at, count)]
            arrived(ref, self.p_recv.at[chunk, half, peer], self.p_send.at[chunk, half, 0], {near: peer})

        def fold(item, carry):
            own = self.sums[start + item, :, self.x] if half == 0 else self.sums[start + item, self.y]
            total = own.astype(F32)
            for peer in peers:
                total = total + box[peer, at + item].astype(F32)
            total_of[at + item] = total.astype(BF16)
            return carry

        lax.fori_loop(0, count, fold, 0)
        for step in ORDER:
            peer = lax.rem(self.here[far] + step, 4)
            self.launch(
                remote(
                    total_of.at[pl.ds(at, count), peer], self.last[half].at[self.here[far], pl.ds(at, count)],
                    self.q_send.at[chunk, half, step], self.q_recv.at[chunk, half, self.here[far]], {far: peer},
                )
            )

    def settle(self, chunk, half):
        near, far = HALVES[half]
        start, count, at = CHUNKS[chunk][half]
        peers = [lax.rem(self.here[far] + step, 4) for step in (1, 2, 3)]
        box, total_of = self.last[half], self.folded[half]
        for peer in peers:
            ref = box.at[peer, pl.ds(at, count)]
            arrived(ref, self.q_recv.at[chunk, half, peer], self.q_send.at[chunk, half, 0], {far: peer})

        def close(item, carry):
            total = total_of[at + item, self.here[far]].astype(F32)
            for peer in peers:
                total = total + box[peer, at + item].astype(F32)
            self.flat[pl.ds(pl.multiple_of((start + item) * 16, 16), 16), :] = total
            return carry

        lax.fori_loop(0, count, close, 0)

    def along_z(self, turn, item, letters, out):
        rows = letters.shape[1]
        for spot in range(8):
            letters[spot] = self.flat[pl.ds(16 * item + spot, rows, stride=8), :].astype(BF16)
        for step in range(1, 8):
            peer = lax.rem(self.z + step, 8)
            self.launch(
                remote(
                    letters.at[peer], out.at[self.z], self.z_send.at[turn, step], self.z_recv.at[turn, self.z],
                    {"dp_1": peer},
                )
            )
        out[self.z] = letters[self.z]

    def collect(self, turn, out):
        for step in range(1, 8):
            peer = lax.rem(self.z + step, 8)
            arrived(out.at[peer], self.z_recv.at[turn, peer], self.z_send.at[turn, 0], {"dp_1": peer})


NN = (((1,), (0,)), ((), ()))
NT = (((1,), (1,)), ((), ()))
TN = (((0,), (0,)), ((), ()))


def dot(a, b, dims=NN):
    return lax.dot_general(a, b, dims, preferred_element_type=F32)


def window_kernel(
    moves, values, rewards, hidden_in, first_in, second_in, head_in, embed_in, early, late,
    first_v, second_v, head_v, embed_v, hidden_v, rows, stage, wide, w, g,
    inbox, sums, a_in, b_in, a_sum, b_sum, a_last, b_last, flat, early_out, late_out,
    xs, hs, bs, zs, xt, bt, state, mixed, pre, summed, saved, local_sem, *sems,
):
    seat = y, z, x, c = seats()
    barrier = greet_all(y, z, x, c)
    pairs = (
        (first_in, first_v), (second_in, second_v), (head_in, head_v), (embed_in, embed_v), (hidden_in, hidden_v)
    )
    loads = [pltpu.make_async_copy(src, dst, local_sem.at[k]) for k, (src, dst) in enumerate(pairs)]
    for load in loads:
        load.start()
    started = []
    gather = Gather(seat, w, stage, wide, sems[0:10], started)
    scatter = Scatter(
        seat, g, (inbox, sums, a_in, b_in, a_sum, b_sum, a_last, b_last, flat), sems[10:18], started
    )
    rows[2 * HEAD : 2 * SECOND, :] = jnp.zeros((10, 128), F32)
    for load in loads[0:4]:
        load.wait()
    for tap in range(9):
        at = 2 * (SECOND + tap)
        rows[at : at + 2, :] = second_v[tap // 3, tap % 3]
        at = 2 * (FIRST + tap)
        rows[at : at + 2, :] = first_v[tap // 3, tap % 3]
    for block in range(5):
        width = min(128, BUCKETS - 128 * block)
        at = 2 * (HEAD + block)
        rows[at : at + 2, 0:width] = head_v[0, :, 128 * block : 128 * block + width]
    for r in range(2):
        at = 2 * EMBED + r
        rows[at : at + 1, :] = jnp.broadcast_to(embed_v[:, r : r + 1], (1, 128))
    stage[z] = rows[...].astype(BF16)
    pl.semaphore_wait(barrier, 14)
    gather.along_z()

    row = lax.broadcasted_iota(jnp.int32, (ROWS, CHANNELS), 0)
    valid = lax.rem(row, PITCH) < SIDE

    def whole(h, item):
        return w[h, item].reshape(CHANNELS, 128)

    def first(tap):
        return jnp.concatenate([whole(0, FIRST + tap), whole(1, FIRST + tap)], axis=1)

    def second(tap):
        return jnp.concatenate([whole(0, SECOND + tap), whole(1, SECOND + tap)], axis=1)

    def head(h):
        return jnp.concatenate([whole(h, HEAD + k) for k in range(5)], axis=1)

    def conv(field, kernel, flip):
        taps = [8 - t if flip else t for t in range(9)]
        lhs = jnp.concatenate(
            [field[t % 3, PITCH * (t // 3) : PITCH * (t // 3) + ROWS] for t in range(9)], axis=1
        )
        return lhs, [kernel(t) for t in taps]

    def conv_plain(field, kernel, flip):
        lhs, parts = conv(field, kernel, flip)
        return dot(lhs, jnp.concatenate(parts, axis=0))

    def conv_swapped(field, kernel, flip):
        lhs, parts = conv(field, kernel, flip)
        return dot(lhs, jnp.concatenate(parts, axis=1), NT)

    def spread(value, dest):
        dest[1, PITCH : PITCH + ROWS] = value.astype(BF16)
        dest[0, PITCH : PITCH + ROWS] = pltpu.roll(value, 1, 0).astype(BF16)
        dest[2, PITCH : PITCH + ROWS] = pltpu.roll(value, ROWS - 1, 0).astype(BF16)

    def turned(value):
        tall = jnp.concatenate([value, jnp.zeros((TALL - ROWS, CHANNELS), F32)], axis=0)
        return tall.T.astype(BF16)

    def total(value):
        return jnp.sum(jnp.sum(value, axis=0, keepdims=True), axis=1, keepdims=True)

    def store(h, item, value):
        g[h, item] = value.astype(BF16).reshape(4, 4, 16, 128)

    for field in (xs, hs, bs, zs):
        for k in range(2):
            for b in range(3):
                field[k, b, 0:PITCH] = jnp.zeros((PITCH, CHANNELS), BF16)
                field[k, b, PITCH + ROWS : DEPTH] = jnp.zeros((DEPTH - PITCH - ROWS, CHANNELS), BF16)
    flat[16 * FIRST : 16 * FIRST + 32, :] = jnp.zeros((32, 128), F32)

    state[...] = jnp.zeros((ROWS, CHANNELS), F32)
    loads[4].wait()

    def place(line, carry):
        cells = hidden_v[line].astype(F32)
        mine = jnp.where(c == 0, cells[:, 0, :], cells[:, 1, :])
        state[pl.ds(pl.multiple_of(PITCH * line, PITCH), SIDE), :] = mine
        return carry

    lax.fori_loop(0, SIDE, place, 0)
    lane = lax.broadcasted_iota(jnp.int32, (CHANNELS, CHANNELS), 1)
    natural = 64 * (lane // 64) + 8 * (lane % 8) + 2 * ((lane // 16) % 4) + (lane // 8) % 2
    source = lax.broadcasted_iota(jnp.int32, (CHANNELS, CHANNELS), 0)
    permute = jnp.where(source == natural, 1.0, 0.0).astype(BF16)
    state[...] = dot(state[...].astype(BF16), permute)

    gather.near_sends()
    for chunk in (2, 1, 0):
        gather.far_sends(chunk)
    for chunk in (2, 1, 0):
        gather.relays(chunk)
    gather.finish(2)

    ones = jnp.ones((16, 128), BF16)
    pick = lax.broadcasted_iota(jnp.int32, (16, 128), 1) == 0
    pick = jnp.where(pick, ones, jnp.zeros_like(ones))
    embed = [dot(pick, whole(e, EMBED), NT)[0:1, :] for e in range(2)]

    bucket = lax.broadcasted_iota(jnp.int32, (16, 640), 1)
    kept = []
    pooled_rows = jnp.zeros((16, CHANNELS), F32)
    grad_rows = [jnp.zeros((16, 640), F32) for _ in range(2)]
    for k in range(2):
        move = moves[c, k]
        spot = PITCH * lax.div(move, SIDE) + lax.rem(move, SIDE)
        passed = move == CELLS
        added = jnp.where(row == spot, embed[0], 0.0) + jnp.where(passed, 1.0, 0.0) * embed[1]
        now = jnp.where(valid, state[...] + added, 0.0)
        mixed[...] = now
        spread(now, xs.at[k])
        xt[:, TALL * k : TALL * k + TALL] = turned(now)
        value = SCALE * conv_plain(xs.at[k], first, False)
        pre[k] = value
        spread(jnp.where(valid, value * jax.nn.sigmoid(value), 0.0), hs.at[k])
        if k == 0:
            gather.finish(1)
        branch = conv_swapped(hs.at[k], second, False)
        value = jnp.where(valid, mixed[...] + SCALE * branch, 0.0)
        summed[k] = value
        factor = lax.rsqrt(total(value * value) / (CELLS * CHANNELS) + eps_norm)
        value = value * factor
        state[...] = value
        if k == 0:
            gather.finish(0)
        pooled = (jnp.sum(value, axis=0, keepdims=True) / CELLS).astype(BF16)
        pooled = jnp.broadcast_to(pooled.astype(F32), (16, CHANNELS))
        own_row = lax.broadcasted_iota(jnp.int32, (16, CHANNELS), 0) == k
        pooled_rows = jnp.where(own_row, pooled, pooled_rows)
        pooled = pooled.astype(BF16)
        pooled_grad = jnp.zeros((16, CHANNELS), F32)
        for h, targets in enumerate((values, rewards)):
            raw = head_scale * dot(pooled, head(h))
            squashed = jnp.tanh(raw / soft_cap)
            raised = jnp.where(bucket < BUCKETS, jnp.exp(soft_cap * squashed), 0.0)
            chances = raised / jnp.sum(raised, axis=1, keepdims=True)
            picked = jnp.where(bucket == targets[c, k], 1.0, 0.0)
            logit = (chances - picked) * (1.0 - squashed * squashed) / 256.0
            logit = jnp.where(bucket < BUCKETS, logit, 0.0).astype(BF16)
            pooled_grad = pooled_grad + dot(logit, head(h), NT)
            logit = logit.astype(F32)
            own_row = lax.broadcasted_iota(jnp.int32, (16, 640), 0) == k
            grad_rows[h] = jnp.where(own_row, logit, grad_rows[h])
        kept.append((spot, passed, factor, head_scale * pooled_grad[0:1, :] / CELLS))

    for h in range(2):
        grad = head_scale * dot(pooled_rows.astype(BF16), grad_rows[h].astype(BF16), TN)
        for block in range(5):
            store(h, HEAD + block, grad[:, 128 * block : 128 * block + 128])
    for half in range(2):
        scatter.to_partner(0, half)

    def window(field, tap):
        start = PITCH * (tap // 3)
        return jnp.concatenate([field[k, tap % 3, start : start + TALL] for k in range(2)], axis=0)

    embed_grad = [jnp.zeros((1, CHANNELS), F32) for _ in range(2)]
    for k in (1, 0):
        spot, passed, factor, pooled_grad = kept[k]
        grad = pooled_grad if k == 1 else saved[...] + pooled_grad
        grad = jnp.where(valid, grad, 0.0)
        value = summed[k]
        slope = total(grad * value) / (CELLS * CHANNELS)
        summed_grad = factor * grad - factor * factor * factor * value * slope
        saved[...] = summed_grad
        spread(summed_grad, bs.at[k])
        bt[:, TALL * k : TALL * k + TALL] = turned(summed_grad)
        if k == 0:
            for tap in range(9):
                grad = SCALE * dot(bt[...], window(hs, tap))
                store(0, SECOND + tap, grad[:, 0:128])
                store(1, SECOND + tap, grad[:, 128:256])
                if tap == 4:
                    scatter.to_partner(1, 0)
            scatter.to_partner(1, 1)
        hidden_grad = SCALE * conv_plain(bs.at[k], second, True)
        for half in range(2):
            scatter.near_sends(1 - k, half)
        value = pre[k]
        sig = jax.nn.sigmoid(value)
        inner = hidden_grad * (sig * (1.0 + value * (1.0 - sig)))
        spread(jnp.where(valid, inner, 0.0), zs.at[k])
        carry = saved[...] + SCALE * conv_swapped(zs.at[k], first, True)
        carry = jnp.where(valid, carry, 0.0)
        saved[...] = carry
        embed_grad[0] = embed_grad[0] + jnp.sum(jnp.where(row == spot, carry, 0.0), axis=0, keepdims=True)
        embed_grad[1] = embed_grad[1] + jnp.where(passed, 1.0, 0.0) * jnp.sum(carry, axis=0, keepdims=True)
        if k == 1:
            for half in range(2):
                scatter.far_sends(0, half)

    for e in range(2):
        lines = jnp.broadcast_to(embed_grad[e], (16, CHANNELS)).astype(BF16)
        top = lax.broadcasted_iota(jnp.int32, (16, 128), 0) == 0
        store(e, EMBED, dot(lines, jnp.where(top, ones, jnp.zeros_like(ones)), TN))

    for tap in range(9):
        grad = SCALE * dot(xt[...], window(zs, 8 - tap))
        store(0, FIRST + tap, grad[:, 0:128])
        store(1, FIRST + tap, grad[:, 128:256])
        if tap == 4:
            scatter.to_partner(2, 0)
    scatter.to_partner(2, 1)
    scatter.near_sends(2, 0)
    for half in range(2):
        scatter.settle(0, half)
        scatter.far_sends(1, half)
    scatter.near_sends(2, 1)
    for half in range(2):
        scatter.settle(1, half)
    scatter.along_z(0, 0, early_out, early)
    for half in range(2):
        scatter.far_sends(2, half)
    for half in range(2):
        scatter.settle(2, half)
    scatter.along_z(1, 12, late_out, late)
    scatter.collect(0, early)
    scatter.collect(1, late)
    for copy in started:
        copy.wait_send()


def window_grads(moves, values, rewards, hidden_state, params):
    vmem = pl.BlockSpec(memory_space=pltpu.VMEM)
    smem = pl.BlockSpec(memory_space=pltpu.SMEM)
    hbm = pl.BlockSpec(memory_space=pltpu.HBM)
    dma = pltpu.SemaphoreType.DMA
    copies = pltpu.VMEM((2, 3, DEPTH, CHANNELS), BF16)
    turned = pltpu.VMEM((CHANNELS, 2 * TALL), BF16)
    field = pltpu.VMEM((ROWS, CHANNELS), F32)
    fields = pltpu.VMEM((2, ROWS, CHANNELS), F32)
    board = pltpu.VMEM((ITEMS, 4, 4, 16, 128), BF16)
    boards = pltpu.VMEM((2, ITEMS, 4, 4, 16, 128), BF16)
    early, late = (8, 32, 128), (8, 24, 128)
    return pl.pallas_call(
        window_kernel,
        out_shape=[jax.ShapeDtypeStruct(early, BF16), jax.ShapeDtypeStruct(late, BF16)],
        in_specs=[smem] * 3 + [hbm] * 5,
        out_specs=[vmem, vmem],
        scratch_shapes=[pltpu.VMEM(p.shape, F32) for p in params]
        + [
            pltpu.VMEM(hidden_state.shape, BF16),
            pltpu.VMEM((48, 128), F32),
            pltpu.VMEM((8, 48, 128), BF16),
            pltpu.VMEM((448, 128), F32),
            boards,
            boards,
            board,
            board,
            pltpu.VMEM((4, 12, 4, 16, 128), BF16),
            pltpu.VMEM((4, 12, 4, 16, 128), BF16),
            pltpu.VMEM((12, 4, 16, 128), BF16),
            pltpu.VMEM((12, 4, 16, 128), BF16),
            pltpu.VMEM((4, 12, 16, 128), BF16),
            pltpu.VMEM((4, 12, 16, 128), BF16),
            pltpu.VMEM((384, 128), F32),
            pltpu.VMEM(early, BF16),
            pltpu.VMEM(late, BF16),
            copies,
            copies,
            copies,
            copies,
            turned,
            turned,
            field,
            field,
            fields,
            fields,
            field,
            dma((5,)),
        ]
        + [
            dma(shape)
            for shape in (
                (8,), (8,), (3, 2, 4), (3, 2, 4), (3, 2, 2), (3, 2, 2), (3, 2, 2), (3, 2, 2), (3, 2, 5), (3, 2, 5),
                (3, 2), (3, 2), (3, 2, 4), (3, 2, 4), (3, 2, 4), (3, 2, 4), (2, 8), (2, 8),
            )
        ],
        compiler_params=pltpu.CompilerParams(
            collective_id=0, has_side_effects=True, vmem_limit_bytes=58 << 20
        ),
        name="window",
    )(moves, values, rewards, hidden_state, *params)


def adam(param, grad, mean, square):
    mean_new = beta_one * mean + (1.0 - beta_one) * grad
    square_new = beta_two * square + (1.0 - beta_two) * grad * grad
    param_new = param - step_size * mean_new / (jnp.sqrt(square_new) + eps_adam)
    return param_new, mean_new, square_new, grad


def adam_kernel(early, late, *refs):
    params, means, squares, outs = refs[0:4], refs[4:8], refs[8:12], refs[12:]
    new, mean_new, square_new, grads = outs[0:4], outs[4:8], outs[8:12], outs[12:16]
    totals = []
    for parts in (early, late):
        total = parts[0].astype(F32)
        for piece in range(1, 8):
            total = total + parts[piece].astype(F32)
        totals.append(total)

    def owned(item):
        if item < FIRST:
            return totals[0][2 * item : 2 * item + 2]
        return totals[1][2 * (item - 12) : 2 * (item - 12) + 2]

    for which in range(2):
        for tap in range(9):
            a, b = tap // 3, tap % 3
            grad = owned((FIRST, SECOND)[which] + tap)
            results = adam(params[which][a, b], grad, means[which][a, b], squares[which][a, b])
            for ref, result in zip((new, mean_new, square_new, grads), results):
                ref[which][a, b] = result
    head = jnp.concatenate([owned(HEAD + k) for k in range(5)], axis=1)[:, 0:BUCKETS]
    results = adam(params[2][0], head, means[2][0], squares[2][0])
    for ref, result in zip((new, mean_new, square_new, grads), results):
        ref[2][0] = result
    embed = owned(EMBED)
    embed = jnp.concatenate([embed[0:1, 0:1], embed[1:2, 0:1]], axis=1)
    results = adam(params[3][...], embed, means[3][...], squares[3][...])
    for ref, result in zip((new, mean_new, square_new, grads), results):
        ref[3][...] = result


def updates(early, late, params, means, squares):
    vmem = pl.BlockSpec(memory_space=pltpu.VMEM)
    shapes = [jax.ShapeDtypeStruct(p.shape, F32) for p in params]
    return pl.pallas_call(
        adam_kernel,
        out_shape=shapes * 4,
        in_specs=[vmem] * 14,
        out_specs=[vmem] * 16,
        compiler_params=pltpu.CompilerParams(vmem_limit_bytes=8 << 20),
        name="adam",
    )(early, late, *params, *means, *squares)


def local(
    hidden_state,
    actions,
    value_target,
    reward_target,
    kernel_first,
    kernel_second,
    head_weight,
    action_embed,
    first_mean,
    first_square,
    second_mean,
    second_square,
    head_mean,
    head_square,
    embed_mean,
    embed_square,
):
    params = (kernel_first, kernel_second, head_weight, action_embed)
    boards = jnp.transpose(hidden_state, (1, 2, 0, 3))
    early, late = window_grads(actions, value_target, reward_target, boards, params)
    outs = updates(
        early,
        late,
        params,
        (first_mean, second_mean, head_mean, embed_mean),
        (first_square, second_square, head_square, embed_square),
    )
    new, means, squares, sums = outs[0:4], outs[4:8], outs[8:12], outs[12:16]
    moments = [moment for pair in zip(means, squares) for moment in pair]
    return (*new, *moments, *sums)


def solution(mesh):
    torus = Mesh(mesh.devices.reshape(4, 8, 4, mesh.shape["mp"]), ("dp_0", "dp_1", "dp_2", "mp"))
    kernel = P(None, None, DP, "mp")
    head = P("mp", DP, None)
    embed = P("mp", DP)
    rows = P(DP, None)
    placed = (P(DP, None, None, None), rows, rows, rows, kernel, kernel, head, embed)
    moments = (kernel, kernel, kernel, kernel, head, head, embed, embed)
    return jax.shard_map(
        local,
        mesh=torus,
        in_specs=placed + moments,
        out_specs=(kernel, kernel, head, embed) + moments + (kernel, kernel, head, embed),
        check_vma=False,
    )
```

time: 89.2 us -> 79.1 us (0.89)
  local copies, waits for them, and re-layouts: 8.19 us -> 2.25 us
  Pallas kernels: 79.4 us -> 75.8 us
    unnamed x37 -> x28, local copies, waits for them, and re-layouts: 8.19 us -> 2.25 us
    pallas_call x4 -> x2, Pallas kernels: 79.4 us -> 75.8 us  [the longest x1 75.1 us: window_grads(): pl.pallas_call(window_kernel, out_shape=[jax.ShapeDtypeStruct(early, BF16...]
where the time goes in v1:
time: 79.1 us; the launch traced here: 78.9 us
  Pallas kernels  75.8 us (96%)
  local copies, waits for them, and re-layouts  2.25 us (3%)
  between operations  0.83 us (1%)
    pallas_call x1, Pallas kernels, window_grads(): pl.pallas_call(window_kernel, out_shape=[jax.ShapeDtypeStruct(early, BF16...  75.1 us
    unnamed x28, local copies, waits for them, and re-layouts  2.25 us

profile of v1, /device:TPU:2, one launch (start us, length us, event | category | flops | bytes accessed | tf_op | source)
XLA Modules:
  0.0 78.9 jit_solution(2094169594217486814)
XLA Ops:
  0.7 0.0 copy-start.2
  0.7 0.0 copy-start.3
  0.7 0.0 copy-start.4
  0.7 0.0 copy-start.5
  0.7 0.0 copy-start.6
  0.7 0.0 copy-start.7
  0.7 0.0 copy-start.8
  0.7 0.0 copy-start.9
  0.7 0.0 copy-start.10
  0.7 75.1 %window.1 = (bf16[8,32,128]{2,1,0:T(8,128)(2,1)}, bf16[8,24,128]{2,1,0:T(8,128)(2,1)}) custom-call(s32[2,2]{1,0:T(2,128)} %moves.1, s32[2,2]{1,0:T(2,128)} %values.1, s32[2,2]{1,0:T(2,128)} %rewards.1, bf16[19,19,2,256]{3,2,1,0:T(2,128)(2,1)} %bitcast.1, f32[3,3,2,128]{3,2,1,0:T(2,128)} %refs_0_.1, f32[3,3,2,128]{3,2,1,0:T(2,128)} %refs_1_.1, ...), custom_call_target="tpu_custom_call" | custom-call | tf_op jit(solution)/shard_map/window/pallas_call | solution.py:566
  75.8 0.0 copy-start.11
  75.8 0.0 copy-start.12
  75.8 0.0 copy-start.13
  75.8 0.0 copy-done.2
  75.9 0.0 copy-done.3
  75.9 0.0 copy-done.4
  75.9 0.0 copy-done.5
  75.9 0.0 copy-done.6
  75.9 0.5 copy-done.11
  76.5 0.0 copy-done.12
  76.5 0.0 copy-done.13
  76.5 0.8 %copy-done = bf16[8,32,128]{2,1,0:T(8,128)(2,1)S(1)} copy-done((bf16[8,32,128]{2,1,0:T(8,128)(2,1)S(1)}, bf16[8,32,128]{2,1,0:T(8,128)(2,1)}, u32[]{:S(2)}) %copy-start) | copy-done | bytes 65560
  77.3 0.8 %copy-done.1 = bf16[8,24,128]{2,1,0:T(8,128)(2,1)S(1)} copy-done((bf16[8,24,128]{2,1,0:T(8,128)(2,1)S(1)}, bf16[8,24,128]{2,1,0:T(8,128)(2,1)}, u32[]{:S(2)}) %copy-start.1) | copy-done | bytes 49176
  78.1 0.7 adam.1
  (6 shorter events, 0.0 us)
Async XLA Ops:
  0.7 75.2 %copy-start.2 = (f32[3,3,2,128]{3,2,1,0:T(2,128)S(1)}, f32[3,3,2,128]{3,2,1,0:T(2,128)}, u32[]{:S(2)}) copy-start(f32[3,3,2,128]{3,2,1,0:T(2,128)} %refs_0_.1) | copy-start | bytes 27652
  0.7 75.2 %copy-start.3 = (f32[3,3,2,128]{3,2,1,0:T(2,128)S(1)}, f32[3,3,2,128]{3,2,1,0:T(2,128)}, u32[]{:S(2)}) copy-start(f32[3,3,2,128]{3,2,1,0:T(2,128)} %refs_1_.1) | copy-start | bytes 27652
  0.7 75.2 %copy-start.4 = (f32[1,2,601]{2,1,0:T(2,128)S(1)}, f32[1,2,601]{2,1,0:T(2,128)}, u32[]{:S(2)}) copy-start(f32[1,2,601]{2,1,0:T(2,128)} %refs_2_.1) | copy-start | bytes 14428
  0.7 75.2 %copy-start.5 = (f32[3,3,2,128]{3,2,1,0:T(2,128)S(1)}, f32[3,3,2,128]{3,2,1,0:T(2,128)}, u32[]{:S(2)}) copy-start(f32[3,3,2,128]{3,2,1,0:T(2,128)} %refs_4_.1) | copy-start | bytes 27652
  0.7 75.2 %copy-start.6 = (f32[3,3,2,128]{3,2,1,0:T(2,128)S(1)}, f32[3,3,2,128]{3,2,1,0:T(2,128)}, u32[]{:S(2)}) copy-start(f32[3,3,2,128]{3,2,1,0:T(2,128)} %refs_5_.1) | copy-start | bytes 27652
  0.7 75.2 %copy-start.7 = (f32[3,3,2,128]{3,2,1,0:T(2,128)S(1)}, f32[3,3,2,128]{3,2,1,0:T(2,128)}, u32[]{:S(2)}) copy-start(f32[3,3,2,128]{3,2,1,0:T(2,128)} %refs_8_.1) | copy-start | bytes 27652
  0.7 75.2 %copy-start.8 = (f32[3,3,2,128]{3,2,1,0:T(2,128)S(1)}, f32[3,3,2,128]{3,2,1,0:T(2,128)}, u32[]{:S(2)}) copy-start(f32[3,3,2,128]{3,2,1,0:T(2,128)} %refs_9_.1) | copy-start | bytes 27652
  0.7 75.2 %copy-start.9 = (f32[1,2,601]{2,1,0:T(2,128)S(1)}, f32[1,2,601]{2,1,0:T(2,128)}, u32[]{:S(2)}) copy-start(f32[1,2,601]{2,1,0:T(2,128)} %refs_6_.1) | copy-start | bytes 14428
  0.7 75.2 %copy-start.10 = (f32[1,2,601]{2,1,0:T(2,128)S(1)}, f32[1,2,601]{2,1,0:T(2,128)}, u32[]{:S(2)}) copy-start(f32[1,2,601]{2,1,0:T(2,128)} %refs_10_.1) | copy-start | bytes 14428
  75.8 0.7 copy-start.11
  75.8 0.7 copy-start.12
  75.8 0.7 copy-start.13
  76.5 0.8 %copy-start = (bf16[8,32,128]{2,1,0:T(8,128)(2,1)S(1)}, bf16[8,32,128]{2,1,0:T(8,128)(2,1)}, u32[]{:S(2)}) copy-start(bf16[8,32,128]{2,1,0:T(8,128)(2,1)} %get-tuple-element.34.early) | copy-start | bytes 196612
  77.3 0.8 %copy-start.1 = (bf16[8,24,128]{2,1,0:T(8,128)(2,1)S(1)}, bf16[8,24,128]{2,1,0:T(8,128)(2,1)}, u32[]{:S(2)}) copy-start(bf16[8,24,128]{2,1,0:T(8,128)(2,1)} %get-tuple-element.35.late) | copy-start | bytes 147460

commit v2 on v1

--- a/solution.py
+++ b/solution.py
@@ -20,7 +20,12 @@
 DEPTH = 704
 ITEMS = 24
 HEAD, SECOND, FIRST, EMBED = 0, 5, 14, 23
-CHUNKS = (((0, 2, 0), (2, 3, 0)), ((5, 5, 2), (10, 4, 3)), ((14, 5, 7), (19, 5, 7)))
+CHUNKS = (((0, 2), (2, 3)), ((5, 5), (10, 4)), ((14, 5), (19, 5)))
+PIECES = (
+    (0, 0, 2, 0), (1, 2, 3, 0),
+    (0, 5, 3, 2), (1, 8, 2, 3), (0, 10, 2, 5), (1, 12, 2, 5),
+    (0, 14, 2, 7), (1, 16, 2, 7), (0, 18, 2, 9), (1, 20, 2, 9), (0, 22, 1, 11), (1, 23, 1, 11),
+)
 HALVES = (("dp_2", "dp_0"), ("dp_0", "dp_2"))
 ORDER = (1, 3, 2)
 SCALE = (9.0 * CHANNELS) ** (-0.5)
@@ -35,6 +40,16 @@
 
 F32 = jnp.float32
 BF16 = jnp.bfloat16
+
+
+def scoped(method):
+    @functools.wraps(method)
+    def inner(self, *given):
+        tag = "_".join(str(v) for v in given if isinstance(v, int))
+        with jax.named_scope(f"{type(self).__name__}_{method.__name__}_{tag}"):
+            return method(self, *given)
+
+    return inner
 
 
 def seats():
@@ -77,7 +92,7 @@
         self.here = {"dp_0": self.y, "dp_2": self.x}
         self.w, self.stage, self.wide, self.started = w, stage, wide, started
         self.z_send, self.z_recv, self.p_send, self.p_recv = sems[0:4]
-        self.q_send, self.q_recv, self.r_send, self.r_recv, self.m_send, self.m_recv = sems[4:10]
+        self.q_send, self.q_recv, self.m_send, self.m_recv = sems[4:8]
         self.partner = {"mp": 1 - self.c}
 
     def launch(self, copy):
@@ -85,106 +100,99 @@
         self.started.append(copy)
 
     def tile(self, chunk, half, near, far):
-        start, count, _ = CHUNKS[chunk][half]
-        items = pl.ds(start, count)
+        items = pl.ds(*CHUNKS[chunk][half])
         if half == 0:
             return self.w.at[self.c, items, far, near]
         return self.w.at[self.c, items, near, far]
 
-    def slab(self, chunk, half, far, core, part=None):
-        start, count, _ = CHUNKS[chunk][half]
-        items = pl.ds(start, count)
-        span = pl.ds(0, 4) if part is None else pl.ds(2 * part, 2)
+    def slab(self, chunk, half, far, core):
+        items = pl.ds(*CHUNKS[chunk][half])
         if half == 0:
-            return self.w.at[core, items, far, span]
-        return self.w.at[core, items, span, far]
-
+            return self.w.at[core, items, far]
+        return self.w.at[core, items, :, far]
+
+    @scoped
     def along_z(self):
         z = self.z
+        for group in (1, 0):
+            ref = self.stage.at[group, z]
+            for step in range(1, 8):
+                peer = {"dp_1": lax.rem(z + step, 8)}
+                self.launch(remote(ref, ref, self.z_send.at[group, step], self.z_recv.at[group, z], peer))
+
+    @scoped
+    def unpack(self, group):
         for step in range(1, 8):
-            peer = {"dp_1": lax.rem(z + step, 8)}
-            ref = self.stage.at[z]
-            self.launch(remote(ref, ref, self.z_send.at[step], self.z_recv.at[z], peer))
-
-    def near_sends(self):
-        z = self.z
-        for step in range(1, 8):
-            peer = lax.rem(z + step, 8)
-            arrived(self.stage.at[peer], self.z_recv.at[peer], self.z_send.at[0], {"dp_1": peer})
+            peer = lax.rem(self.z + step, 8)
+            sems = self.z_recv.at[group, peer], self.z_send.at[group, 0]
+            arrived(self.stage.at[group, peer], *sems, {"dp_1": peer})
         for piece in range(8):
-            self.wide[56 * piece : 56 * piece + 48, :] = self.stage[piece].astype(F32)
-        for chunk in (2, 1, 0):
+            self.wide[group, 24 * piece : 24 * piece + 24, :] = self.stage[group, piece].astype(F32)
+
+    def to_far(self, chunk, half, turn, near):
+        far = HALVES[half][1]
+        at = self.here[far]
+        ref = self.tile(chunk, half, near, at)
+        for step in ORDER:
+            self.launch(
+                remote(
+                    ref, ref, self.q_send.at[chunk, half, turn, step], self.q_recv.at[chunk, half, at],
+                    {far: lax.rem(at + step, 4)},
+                )
+            )
+
+    @scoped
+    def near_sends(self, chunk):
+        for half, (near, far) in enumerate(HALVES):
+            start, count = CHUNKS[chunk][half]
+            for item in range(start, start + count):
+                group, line = item // 12, 2 * (item % 12)
+                slab = self.wide.at[group]
+                low = slab[pl.ds(line, 8, stride=24), :]
+                high = slab[pl.ds(line + 1, 8, stride=24), :]
+                self.w[self.c, item, self.y, self.x] = jnp.concatenate([low, high], axis=0).astype(BF16)
+        for step in ORDER:
             for half, (near, far) in enumerate(HALVES):
-                start, count, _ = CHUNKS[chunk][half]
-                for item in range(start, start + count):
-                    low = self.wide[pl.ds(2 * item, 8, stride=56), :]
-                    high = self.wide[pl.ds(2 * item + 1, 8, stride=56), :]
-                    block = jnp.concatenate([low, high], axis=0).astype(BF16)
-                    self.w[self.c, item, self.y, self.x] = block
-            for step in ORDER:
-                for half, (near, far) in enumerate(HALVES):
-                    at = self.here[near]
-                    ref = self.tile(chunk, half, at, self.here[far])
-                    self.launch(
-                        remote(
-                            ref, ref, self.p_send.at[chunk, half, step], self.p_recv.at[chunk, half, at],
-                            {near: lax.rem(at + step, 4)},
-                        )
+                at = self.here[near]
+                ref = self.tile(chunk, half, at, self.here[far])
+                self.launch(
+                    remote(
+                        ref, ref, self.p_send.at[chunk, half, step], self.p_recv.at[chunk, half, at],
+                        {near: lax.rem(at + step, 4)},
                     )
-
-    def to_partner(self, chunk, half, piece, ref):
-        self.launch(
-            remote(
-                ref, ref, self.m_send.at[chunk, half, piece], self.m_recv.at[chunk, half, piece], self.partner
-            )
-        )
-
+                )
+
+    def own_sends(self, chunk):
+        for half, (near, far) in enumerate(HALVES):
+            self.to_far(chunk, half, 0, self.here[near])
+
+    def to_partner(self, chunk, half, turn, ref):
+        sems = self.m_send.at[chunk, half, turn], self.m_recv.at[chunk, half, turn]
+        self.launch(remote(ref, ref, *sems, self.partner))
+
+    @scoped
     def far_sends(self, chunk):
-        for half, (near, far) in enumerate(HALVES):
-            for step in ORDER:
+        for step in ORDER:
+            for half, (near, far) in enumerate(HALVES):
                 peer = lax.rem(self.here[near] + step, 4)
                 ref = self.tile(chunk, half, peer, self.here[far])
                 arrived(ref, self.p_recv.at[chunk, half, peer], self.p_send.at[chunk, half, 0], {near: peer})
-            at = self.here[far]
-            ref = self.slab(chunk, half, at, self.c)
-            for way, step in enumerate((1, 3)):
-                self.launch(
-                    remote(
-                        ref, ref, self.q_send.at[chunk, half, way], self.q_recv.at[chunk, half, way],
-                        {far: lax.rem(at + step, 4)},
-                    )
-                )
-            self.to_partner(chunk, half, 0, ref)
-
-    def relays(self, chunk):
+                self.to_far(chunk, half, step, peer)
         for half, (near, far) in enumerate(HALVES):
-            at = self.here[far]
-            for way, (step, back) in enumerate(((1, 3), (3, 1))):
-                peer = lax.rem(at + back, 4)
+            self.to_partner(chunk, half, 0, self.slab(chunk, half, self.here[far], self.c))
+
+    @scoped
+    def finish(self, chunk):
+        for step in ORDER:
+            for half, (near, far) in enumerate(HALVES):
+                peer = lax.rem(self.here[far] + step, 4)
                 ref = self.slab(chunk, half, peer, self.c)
-                arrived(ref, self.q_recv.at[chunk, half, way], self.q_send.at[chunk, half, way], {far: peer})
-                part = self.slab(chunk, half, peer, self.c, way)
-                self.launch(
-                    remote(
-                        part, part, self.r_send.at[chunk, half, way], self.r_recv.at[chunk, half, way],
-                        {far: lax.rem(at + step, 4)},
-                    )
-                )
-                self.to_partner(chunk, half, 1 + way, ref)
-
-    def finish(self, chunk):
+                arrived(ref, self.q_recv.at[chunk, half, peer], self.q_send.at[chunk, half, 0, 0], {far: peer})
+                self.to_partner(chunk, half, step, ref)
         for half, (near, far) in enumerate(HALVES):
-            peer = lax.rem(self.here[far] + 2, 4)
-            for way in range(2):
-                part = self.slab(chunk, half, peer, self.c, way)
-                arrived(part, self.r_recv.at[chunk, half, way], self.r_send.at[chunk, half, way], {far: peer})
-                self.to_partner(chunk, half, 3 + way, part)
-        for half, (near, far) in enumerate(HALVES):
-            at, other = self.here[far], 1 - self.c
-            refs = [self.slab(chunk, half, lax.rem(at + step, 4), other) for step in (0, 3, 1)]
-            refs += [self.slab(chunk, half, lax.rem(at + 2, 4), other, way) for way in range(2)]
-            for piece, ref in enumerate(refs):
-                sems = self.m_recv.at[chunk, half, piece], self.m_send.at[chunk, half, piece]
+            for turn in range(4):
+                ref = self.slab(chunk, half, lax.rem(self.here[far] + turn, 4), 1 - self.c)
+                sems = self.m_recv.at[chunk, half, turn], self.m_send.at[chunk, half, turn]
                 arrived(ref, *sems, self.partner)
 
 
@@ -203,84 +211,76 @@
         copy.start()
         self.started.append(copy)
 
-    def across(self, chunk, half):
-        start, count, _ = CHUNKS[chunk][half]
+    def across(self, piece):
+        half, start, count, _ = PIECES[piece]
         items = pl.ds(start, count)
         return remote(
-            self.g.at[1 - self.c, items], self.inbox.at[items], self.m_send.at[chunk, half],
-            self.m_recv.at[chunk, half], self.partner,
+            self.g.at[1 - self.c, items], self.inbox.at[items], self.m_send.at[piece], self.m_recv.at[piece],
+            self.partner,
         )
 
-    def to_partner(self, chunk, half):
-        self.launch(self.across(chunk, half))
-
-    def near_sends(self, chunk, half):
+    def to_partner(self, piece):
+        self.launch(self.across(piece))
+
+    @scoped
+    def near_sends(self, piece):
+        half, start, count, at = PIECES[piece]
         near, far = HALVES[half]
-        start, count, at = CHUNKS[chunk][half]
-        self.across(chunk, half).wait_recv()
-
-        def join(item, carry):
+        self.across(piece).wait_recv()
+        for item in range(start, start + count):
             total = self.g[self.c, item].astype(F32) + self.inbox[item].astype(F32)
             self.sums[item] = total.astype(BF16)
-            return carry
-
-        lax.fori_loop(start, start + count, join, 0)
         items = pl.ds(start, count)
         for step in ORDER:
             peer = lax.rem(self.here[near] + step, 4)
             ref = self.sums.at[items, :, peer] if half == 0 else self.sums.at[items, peer]
             self.launch(
                 remote(
-                    ref, self.arrivals[half].at[self.here[near], pl.ds(at, count)],
-                    self.p_send.at[chunk, half, step], self.p_recv.at[chunk, half, self.here[near]], {near: peer},
+                    ref, self.arrivals[half].at[self.here[near], pl.ds(at, count)], self.p_send.at[piece, step],
+                    self.p_recv.at[piece, self.here[near]], {near: peer},
                 )
             )
 
-    def far_sends(self, chunk, half):
+    @scoped
+    def far_sends(self, piece):
+        half, start, count, at = PIECES[piece]
         near, far = HALVES[half]
-        start, count, at = CHUNKS[chunk][half]
-        peers = [lax.rem(self.here[near] + step, 4) for step in (1, 2, 3)]
+        peers = [lax.rem(self.here[near] + step, 4) for step in ORDER]
         box, total_of = self.arrivals[half], self.folded[half]
         for peer in peers:
             ref = box.at[peer, pl.ds(at, count)]
-            arrived(ref, self.p_recv.at[chunk, half, peer], self.p_send.at[chunk, half, 0], {near: peer})
-
-        def fold(item, carry):
+            arrived(ref, self.p_recv.at[piece, peer], self.p_send.at[piece, 0], {near: peer})
+        for item in range(count):
             own = self.sums[start + item, :, self.x] if half == 0 else self.sums[start + item, self.y]
             total = own.astype(F32)
             for peer in peers:
                 total = total + box[peer, at + item].astype(F32)
             total_of[at + item] = total.astype(BF16)
-            return carry
-
-        lax.fori_loop(0, count, fold, 0)
         for step in ORDER:
             peer = lax.rem(self.here[far] + step, 4)
             self.launch(
                 remote(
                     total_of.at[pl.ds(at, count), peer], self.last[half].at[self.here[far], pl.ds(at, count)],
-                    self.q_send.at[chunk, half, step], self.q_recv.at[chunk, half, self.here[far]], {far: peer},
+                    self.q_send.at[piece, step], self.q_recv.at[piece, self.here[far]], {far: peer},
                 )
             )
 
-    def settle(self, chunk, half):
+    @scoped
+    def settle(self, piece):
+        half, start, count, at = PIECES[piece]
         near, far = HALVES[half]
-        start, count, at = CHUNKS[chunk][half]
-        peers = [lax.rem(self.here[far] + step, 4) for step in (1, 2, 3)]
+        peers = [lax.rem(self.here[far] + step, 4) for step in ORDER]
         box, total_of = self.last[half], self.folded[half]
         for peer in peers:
             ref = box.at[peer, pl.ds(at, count)]
-            arrived(ref, self.q_recv.at[chunk, half, peer], self.q_send.at[chunk, half, 0], {far: peer})
-
-        def close(item, carry):
+            arrived(ref, self.q_recv.at[piece, peer], self.q_send.at[piece, 0], {far: peer})
+        for item in range(count):
             total = total_of[at + item, self.here[far]].astype(F32)
             for peer in peers:
                 total = total + box[peer, at + item].astype(F32)
-            self.flat[pl.ds(pl.multiple_of((start + item) * 16, 16), 16), :] = total
-            return carry
-
-        lax.fori_loop(0, count, close, 0)
-
+            self.flat[16 * (start + item) : 16 * (start + item) + 16, :] = total
+
+    @scoped
     def along_z(self, turn, item, letters, out):
         rows = letters.shape[1]
         for spot in range(8):
@@ -295,6 +295,7 @@
             )
         out[self.z] = letters[self.z]
 
+    @scoped
     def collect(self, turn, out):
         for step in range(1, 8):
             peer = lax.rem(self.z + step, 8)
@@ -325,9 +326,9 @@
     for load in loads:
         load.start()
     started = []
-    gather = Gather(seat, w, stage, wide, sems[0:10], started)
+    gather = Gather(seat, w, stage, wide, sems[0:8], started)
     scatter = Scatter(
-        seat, g, (inbox, sums, a_in, b_in, a_sum, b_sum, a_last, b_last, flat), sems[10:18], started
+        seat, g, (inbox, sums, a_in, b_in, a_sum, b_sum, a_last, b_last, flat), sems[8:16], started
     )
     rows[2 * HEAD : 2 * SECOND, :] = jnp.zeros((10, 128), F32)
     for load in loads[0:4]:
@@ -344,9 +345,18 @@
     for r in range(2):
         at = 2 * EMBED + r
         rows[at : at + 1, :] = jnp.broadcast_to(embed_v[:, r : r + 1], (1, 128))
-    stage[z] = rows[...].astype(BF16)
-    pl.semaphore_wait(barrier, 14)
+    for group in range(2):
+        stage[group, z] = rows[24 * group : 24 * group + 24, :].astype(BF16)
+    with jax.named_scope("barrier"):
+        pl.semaphore_wait(barrier, 14)
     gather.along_z()
+
+    def phase(run):
+        def inner(*given):
+            with jax.named_scope(run.__name__):
+                return run(*given)
+
+        return inner
 
     row = lax.broadcasted_iota(jnp.int32, (ROWS, CHANNELS), 0)
     valid = lax.rem(row, PITCH) < SIDE
@@ -370,19 +380,25 @@
         )
         return lhs, [kernel(t) for t in taps]
 
+    @phase
     def conv_plain(field, kernel, flip):
         lhs, parts = conv(field, kernel, flip)
-        return dot(lhs, jnp.concatenate(parts, axis=0))
-
+        rhs = jnp.concatenate(parts, axis=0)
+        return jnp.concatenate([dot(lhs[: ROWS // 2], rhs), dot(lhs[ROWS // 2 :], rhs)], axis=0)
+
+    @phase
     def conv_swapped(field, kernel, flip):
         lhs, parts = conv(field, kernel, flip)
-        return dot(lhs, jnp.concatenate(parts, axis=1), NT)
-
+        rhs = jnp.concatenate(parts, axis=1)
+        return jnp.concatenate([dot(lhs[: ROWS // 2], rhs, NT), dot(lhs[ROWS // 2 :], rhs, NT)], axis=0)
+
+    @phase
     def spread(value, dest):
         dest[1, PITCH : PITCH + ROWS] = value.astype(BF16)
         dest[0, PITCH : PITCH + ROWS] = pltpu.roll(value, 1, 0).astype(BF16)
         dest[2, PITCH : PITCH + ROWS] = pltpu.roll(value, ROWS - 1, 0).astype(BF16)
 
+    @phase
     def turned(value):
         tall = jnp.concatenate([value, jnp.zeros((TALL - ROWS, CHANNELS), F32)], axis=0)
         return tall.T.astype(BF16)
@@ -409,18 +425,24 @@
         state[pl.ds(pl.multiple_of(PITCH * line, PITCH), SIDE), :] = mine
         return carry
 
-    lax.fori_loop(0, SIDE, place, 0)
+    with jax.named_scope("place"):
+        lax.fori_loop(0, SIDE, place, 0)
     lane = lax.broadcasted_iota(jnp.int32, (CHANNELS, CHANNELS), 1)
     natural = 64 * (lane // 64) + 8 * (lane % 8) + 2 * ((lane // 16) % 4) + (lane // 8) % 2
     source = lax.broadcasted_iota(jnp.int32, (CHANNELS, CHANNELS), 0)
     permute = jnp.where(source == natural, 1.0, 0.0).astype(BF16)
     state[...] = dot(state[...].astype(BF16), permute)
 
-    gather.near_sends()
-    for chunk in (2, 1, 0):
+    gather.unpack(1)
+    gather.near_sends(2)
+    gather.own_sends(2)
+    gather.unpack(0)
+    gather.near_sends(1)
+    gather.near_sends(0)
+    gather.far_sends(2)
+    for chunk in (1, 0):
+        gather.own_sends(chunk)
         gather.far_sends(chunk)
-    for chunk in (2, 1, 0):
-        gather.relays(chunk)
     gather.finish(2)
 
     ones = jnp.ones((16, 128), BF16)
@@ -428,10 +450,8 @@
     pick = jnp.where(pick, ones, jnp.zeros_like(ones))
     embed = [dot(pick, whole(e, EMBED), NT)[0:1, :] for e in range(2)]
 
-    bucket = lax.broadcasted_iota(jnp.int32, (16, 640), 1)
     kept = []
     pooled_rows = jnp.zeros((16, CHANNELS), F32)
-    grad_rows = [jnp.zeros((16, 640), F32) for _ in range(2)]
     for k in range(2):
         move = moves[c, k]
         spot = PITCH * lax.div(move, SIDE) + lax.rem(move, SIDE)
@@ -452,43 +472,58 @@
         factor = lax.rsqrt(total(value * value) / (CELLS * CHANNELS) + eps_norm)
         value = value * factor
         state[...] = value
-        if k == 0:
-            gather.finish(0)
-        pooled = (jnp.sum(value, axis=0, keepdims=True) / CELLS).astype(BF16)
-        pooled = jnp.broadcast_to(pooled.astype(F32), (16, CHANNELS))
+        pooled = jnp.sum(value, axis=0, keepdims=True) / CELLS
         own_row = lax.broadcasted_iota(jnp.int32, (16, CHANNELS), 0) == k
         pooled_rows = jnp.where(own_row, pooled, pooled_rows)
-        pooled = pooled.astype(BF16)
-        pooled_grad = jnp.zeros((16, CHANNELS), F32)
-        for h, targets in enumerate((values, rewards)):
-            raw = head_scale * dot(pooled, head(h))
-            squashed = jnp.tanh(raw / soft_cap)
-            raised = jnp.where(bucket < BUCKETS, jnp.exp(soft_cap * squashed), 0.0)
-            chances = raised / jnp.sum(raised, axis=1, keepdims=True)
-            picked = jnp.where(bucket == targets[c, k], 1.0, 0.0)
-            logit = (chances - picked) * (1.0 - squashed * squashed) / 256.0
-            logit = jnp.where(bucket < BUCKETS, logit, 0.0).astype(BF16)
-            pooled_grad = pooled_grad + dot(logit, head(h), NT)
-            logit = logit.astype(F32)
-            own_row = lax.broadcasted_iota(jnp.int32, (16, 640), 0) == k
-            grad_rows[h] = jnp.where(own_row, logit, grad_rows[h])
-        kept.append((spot, passed, factor, head_scale * pooled_grad[0:1, :] / CELLS))
-
+        kept.append((spot, passed, factor))
+    gather.finish(0)
+
+    bucket = lax.broadcasted_iota(jnp.int32, (16, 640), 1)
+    top_row = lax.broadcasted_iota(jnp.int32, (16, 640), 0) == 0
+    pooled = pooled_rows.astype(BF16)
+    pooled_grads = jnp.zeros((16, CHANNELS), F32)
+    logits = []
+    for h, targets in enumerate((values, rewards)):
+        raw = head_scale * dot(pooled, head(h))
+        squashed = jnp.tanh(raw / soft_cap)
+        raised = jnp.where(bucket < BUCKETS, jnp.exp(soft_cap * squashed), 0.0)
+        chances = raised / jnp.sum(raised, axis=1, keepdims=True)
+        picked = jnp.where(bucket == jnp.where(top_row, targets[c, 0], targets[c, 1]), 1.0, 0.0)
+        logit = (chances - picked) * (1.0 - squashed * squashed) / 256.0
+        logit = jnp.where(bucket < BUCKETS, logit, 0.0).astype(BF16)
+        pooled_grads = pooled_grads + dot(logit, head(h), NT)
+        logits.append(logit)
     for h in range(2):
-        grad = head_scale * dot(pooled_rows.astype(BF16), grad_rows[h].astype(BF16), TN)
+        grad = head_scale * dot(pooled, logits[h], TN)
         for block in range(5):
             store(h, HEAD + block, grad[:, 128 * block : 128 * block + 128])
-    for half in range(2):
-        scatter.to_partner(0, half)
+    for piece in (0, 1):
+        scatter.to_partner(piece)
 
     def window(field, tap):
         start = PITCH * (tap // 3)
         return jnp.concatenate([field[k, tap % 3, start : start + TALL] for k in range(2)], axis=0)
 
+    def second_taps(*taps):
+        with jax.named_scope("second_taps"):
+            for tap in taps:
+                grad = SCALE * dot(bt[...], window(hs, tap))
+                store(0, SECOND + tap, grad[:, 0:128])
+                store(1, SECOND + tap, grad[:, 128:256])
+
+    def first_taps(*taps):
+        with jax.named_scope("first_taps"):
+            for tap in taps:
+                grad = SCALE * dot(xt[...], window(zs, 8 - tap))
+                store(0, FIRST + tap, grad[:, 0:128])
+                store(1, FIRST + tap, grad[:, 128:256])
+
     embed_grad = [jnp.zeros((1, CHANNELS), F32) for _ in range(2)]
     for k in (1, 0):
-        spot, passed, factor, pooled_grad = kept[k]
-        grad = pooled_grad if k == 1 else saved[...] + pooled_grad
+        spot, passed, factor = kept[k]
+        grad = head_scale * pooled_grads[k : k + 1, :] / CELLS
+        if k == 0:
+            grad = saved[...] + grad
         grad = jnp.where(valid, grad, 0.0)
         value = summed[k]
         slope = total(grad * value) / (CELLS * CHANNELS)
@@ -497,58 +532,70 @@
         spread(summed_grad, bs.at[k])
         bt[:, TALL * k : TALL * k + TALL] = turned(summed_grad)
         if k == 0:
-            for tap in range(9):
-                grad = SCALE * dot(bt[...], window(hs, tap))
-                store(0, SECOND + tap, grad[:, 0:128])
-                store(1, SECOND + tap, grad[:, 128:256])
-                if tap == 4:
-                    scatter.to_partner(1, 0)
-            scatter.to_partner(1, 1)
+            second_taps(0, 1, 2)
+            scatter.to_partner(2)
+            second_taps(3, 4)
+            scatter.to_partner(3)
+            second_taps(5, 6)
+            scatter.to_partner(4)
+            scatter.near_sends(2)
+            second_taps(7, 8)
+            scatter.to_partner(5)
+            scatter.near_sends(3)
         hidden_grad = SCALE * conv_plain(bs.at[k], second, True)
-        for half in range(2):
-            scatter.near_sends(1 - k, half)
+        for piece in ((4, 5), (0, 1))[k]:
+            scatter.near_sends(piece)
         value = pre[k]
         sig = jax.nn.sigmoid(value)
         inner = hidden_grad * (sig * (1.0 + value * (1.0 - sig)))
         spread(jnp.where(valid, inner, 0.0), zs.at[k])
+        if k == 0:
+            first_taps(0, 1)
+            scatter.to_partner(6)
+            first_taps(2, 3)
+            scatter.to_partner(7)
+            first_taps(4, 5)
+            scatter.to_partner(8)
+            scatter.near_sends(6)
+            first_taps(6, 7)
+            scatter.to_partner(9)
+            scatter.near_sends(7)
+            first_taps(8)
+            scatter.to_partner(10)
+            scatter.near_sends(8)
+            scatter.near_sends(9)
         carry = saved[...] + SCALE * conv_swapped(zs.at[k], first, True)
+        if k == 0:
+            scatter.near_sends(10)
         carry = jnp.where(valid, carry, 0.0)
         saved[...] = carry
         embed_grad[0] = embed_grad[0] + jnp.sum(jnp.where(row == spot, carry, 0.0), axis=0, keepdims=True)
         embed_grad[1] = embed_grad[1] + jnp.where(passed, 1.0, 0.0) * jnp.sum(carry, axis=0, keepdims=True)
-        if k == 1:
-            for half in range(2):
-                scatter.far_sends(0, half)
 
     for e in range(2):
         lines = jnp.broadcast_to(embed_grad[e], (16, CHANNELS)).astype(BF16)
         top = lax.broadcasted_iota(jnp.int32, (16, 128), 0) == 0
         store(e, EMBED, dot(lines, jnp.where(top, ones, jnp.zeros_like(ones)), TN))
-
-    for tap in range(9):
-        grad = SCALE * dot(xt[...], window(zs, 8 - tap))
-        store(0, FIRST + tap, grad[:, 0:128])
-        store(1, FIRST + tap, grad[:, 128:256])
-        if tap == 4:
-            scatter.to_partner(2, 0)
-    scatter.to_partner(2, 1)
-    scatter.near_sends(2, 0)
-    for half in range(2):
-        scatter.settle(0, half)
-        scatter.far_sends(1, half)
-    scatter.near_sends(2, 1)
-    for half in range(2):
-        scatter.settle(1, half)
+    scatter.to_partner(11)
+    for piece in (0, 1, 2, 3):
+        scatter.far_sends(piece)
+    scatter.near_sends(11)
+    for piece in (4, 5, 6, 7, 8, 9, 10):
+        scatter.far_sends(piece)
+    for piece in (0, 1, 2, 3):
+        scatter.settle(piece)
+    scatter.far_sends(11)
+    for piece in (4, 5):
+        scatter.settle(piece)
     scatter.along_z(0, 0, early_out, early)
-    for half in range(2):
-        scatter.far_sends(2, half)
-    for half in range(2):
-        scatter.settle(2, half)
+    for piece in (6, 7, 8, 9, 10, 11):
+        scatter.settle(piece)
     scatter.along_z(1, 12, late_out, late)
     scatter.collect(0, early)
     scatter.collect(1, late)
-    for copy in started:
-        copy.wait_send()
+    with jax.named_scope("drain"):
+        for copy in started:
+            copy.wait_send()
 
 
 def window_grads(moves, values, rewards, hidden_state, params):
@@ -572,8 +619,8 @@
         + [
             pltpu.VMEM(hidden_state.shape, BF16),
             pltpu.VMEM((48, 128), F32),
-            pltpu.VMEM((8, 48, 128), BF16),
-            pltpu.VMEM((448, 128), F32),
+            pltpu.VMEM((2, 8, 24, 128), BF16),
+            pltpu.VMEM((2, 192, 128), F32),
             boards,
             boards,
             board,
@@ -603,8 +650,8 @@
         + [
             dma(shape)
             for shape in (
-                (8,), (8,), (3, 2, 4), (3, 2, 4), (3, 2, 2), (3, 2, 2), (3, 2, 2), (3, 2, 2), (3, 2, 5), (3, 2, 5),
-                (3, 2), (3, 2), (3, 2, 4), (3, 2, 4), (3, 2, 4), (3, 2, 4), (2, 8), (2, 8),
+                (2, 8), (2, 8), (3, 2, 4), (3, 2, 4), (3, 2, 4, 4), (3, 2, 4), (3, 2, 4), (3, 2, 4),
+                (12,), (12,), (12, 4), (12, 4), (12, 4), (12, 4), (2, 8), (2, 8),
             )
         ],
         compiler_params=pltpu.CompilerParams(
@@ -621,8 +668,15 @@
     return param_new, mean_new, square_new, grad
 
 
-def adam_kernel(early, late, *refs):
-    params, means, squares, outs = refs[0:4], refs[4:8], refs[8:12], refs[12:]
+def adam_kernel(*refs):
+    given, outs, held, sem = refs[0:14], refs[14:30], refs[30:44], refs[44]
+    loads = [pltpu.make_async_copy(src, dst, sem.at[k]) for k, (src, dst) in enumerate(zip(given, held))]
+    for load in loads:
+        load.start()
+    for load in loads:
+        load.wait()
+    early, late = held[0:2]
+    params, means, squares = held[2:6], held[6:10], held[10:14]
     new, mean_new, square_new, grads = outs[0:4], outs[4:8], outs[8:12], outs[12:16]
     totals = []
     for parts in (early, late):
@@ -657,14 +711,16 @@
 def updates(early, late, params, means, squares):
     vmem = pl.BlockSpec(memory_space=pltpu.VMEM)
     shapes = [jax.ShapeDtypeStruct(p.shape, F32) for p in params]
+    given = (early, late, *params, *means, *squares)
     return pl.pallas_call(
         adam_kernel,
         out_shape=shapes * 4,
-        in_specs=[vmem] * 14,
+        in_specs=[pl.BlockSpec(memory_space=pltpu.HBM)] * 14,
         out_specs=[vmem] * 16,
-        compiler_params=pltpu.CompilerParams(vmem_limit_bytes=8 << 20),
+        scratch_shapes=[pltpu.VMEM(a.shape, a.dtype) for a in given] + [pltpu.SemaphoreType.DMA((14,))],
+        compiler_params=pltpu.CompilerParams(vmem_limit_bytes=58 << 20),
         name="adam",
-    )(early, late, *params, *means, *squares)
+    )(*given)
 
 
 def local(

time: 79.1 us -> 66.2 us (0.84)
  Pallas kernels: 75.8 us -> 65.4 us
  local copies, waits for them, and re-layouts: 2.25 us -> 0 us
    pallas_call x1, Pallas kernels: 75.1 us -> 63.6 us  [window_grads(): pl.pallas_call(window_kernel, out_shape=[jax.ShapeDtypeStruct(early, BF16...]
    unnamed x28 -> x0, local copies, waits for them, and re-layouts: 2.25 us -> none
    pallas_call x1, Pallas kernels: 0.72 us -> 1.79 us  [updates(): pl.pallas_call(adam_kernel, out_shape=shapes * 4, in_specs=[pl.BlockSpec(...]
where the time goes in v2:
time: 66.2 us; the launch traced here: 66 us
  Pallas kernels  65.4 us (99%)
    pallas_call x1, Pallas kernels, window_grads(): pl.pallas_call(window_kernel, out_shape=[jax.ShapeDtypeStruct(early, BF16...  63.6 us
    pallas_call x1, Pallas kernels, updates(): pl.pallas_call(adam_kernel, out_shape=shapes * 4, in_specs=[pl.BlockSpec(...  1.79 us

profile of v2, /device:TPU:2, one launch (start us, length us, event | category | flops | bytes accessed | tf_op | source)
XLA Modules:
  0.0 66.0 jit_solution(10262698535013232735)
XLA Ops:
  0.6 63.6 %window.1 = (bf16[8,32,128]{2,1,0:T(8,128)(2,1)}, bf16[8,24,128]{2,1,0:T(8,128)(2,1)}) custom-call(s32[2,2]{1,0:T(2,128)} %moves.1, s32[2,2]{1,0:T(2,128)} %values.1, s32[2,2]{1,0:T(2,128)} %rewards.1, bf16[19,19,2,256]{3,2,1,0:T(2,128)(2,1)} %bitcast.1, f32[3,3,2,128]{3,2,1,0:T(2,128)} %refs_2_.1, f32[3,3,2,128]{3,2,1,0:T(2,128)} %refs_3_.1, ...), custom_call_target="tpu_custom_call" | custom-call | tf_op jit(solution)/shard_map/window/pallas_call | solution.py:613
  64.2 1.8 %adam.1 = (f32[3,3,2,128]{3,2,1,0:T(2,128)}, f32[3,3,2,128]{3,2,1,0:T(2,128)}, f32[1,2,601]{2,1,0:T(2,128)}, f32[1,2]{1,0:T(1,128)}, f32[3,3,2,128]{3,2,1,0:T(2,...) custom-call(bf16[8,32,128]{2,1,0:T(8,128)(2,1)} %get-tuple-element.3, ...), custom_call_target="tpu_custom_call" | custom-call | tf_op jit(solution)/shard_map/adam/pallas_call | solution.py:715

commit v3 on v2

--- a/solution.py
+++ b/solution.py
@@ -14,10 +14,10 @@
 SIDE = 19
 CELLS = 361
 BUCKETS = 601
-PITCH = 32
-ROWS = SIDE * PITCH
-TALL = 640
-DEPTH = 704
+PITCH = 20
+ROWS = 384
+GUARD = 24
+SHIFTS = tuple(PITCH * (t // 3 - 1) + t % 3 - 1 for t in range(9))
 ITEMS = 24
 HEAD, SECOND, FIRST, EMBED = 0, 5, 14, 23
 CHUNKS = (((0, 2), (2, 3)), ((5, 5), (10, 4)), ((14, 5), (19, 5)))
@@ -182,13 +182,16 @@
             self.to_partner(chunk, half, 0, self.slab(chunk, half, self.here[far], self.c))
 
     @scoped
-    def finish(self, chunk):
+    def cross(self, chunk):
         for step in ORDER:
             for half, (near, far) in enumerate(HALVES):
                 peer = lax.rem(self.here[far] + step, 4)
                 ref = self.slab(chunk, half, peer, self.c)
                 arrived(ref, self.q_recv.at[chunk, half, peer], self.q_send.at[chunk, half, 0, 0], {far: peer})
                 self.to_partner(chunk, half, step, ref)
+
+    @scoped
+    def join(self, chunk):
         for half, (near, far) in enumerate(HALVES):
             for turn in range(4):
                 ref = self.slab(chunk, half, lax.rem(self.here[far] + turn, 4), 1 - self.c)
@@ -312,21 +315,22 @@
 
 
 def window_kernel(
-    moves, values, rewards, hidden_in, first_in, second_in, head_in, embed_in, early, late,
+    moves_in, values_in, rewards_in, hidden_in, first_in, second_in, head_in, embed_in, early, late,
     first_v, second_v, head_v, embed_v, hidden_v, rows, stage, wide, w, g,
     inbox, sums, a_in, b_in, a_sum, b_sum, a_last, b_last, flat, early_out, late_out,
-    xs, hs, bs, zs, xt, bt, state, mixed, pre, summed, saved, local_sem, *sems,
+    xs, hs, bs, zs, xt, bt, state, mixed, pre, summed, saved, slabs, first_t, second_t, moves, values, rewards, local_sem, *sems,
 ):
     seat = y, z, x, c = seats()
     barrier = greet_all(y, z, x, c)
     pairs = (
-        (first_in, first_v), (second_in, second_v), (head_in, head_v), (embed_in, embed_v), (hidden_in, hidden_v)
+        (first_in, first_v), (second_in, second_v), (head_in, head_v), (embed_in, embed_v), (hidden_in, hidden_v),
+        (moves_in, moves), (values_in, values), (rewards_in, rewards),
     )
     loads = [pltpu.make_async_copy(src, dst, local_sem.at[k]) for k, (src, dst) in enumerate(pairs)]
     for load in loads:
         load.start()
-    started = []
-    gather = Gather(seat, w, stage, wide, sems[0:8], started)
+    started, sent = [], []
+    gather = Gather(seat, w, stage, wide, sems[0:8], sent)
     scatter = Scatter(
         seat, g, (inbox, sums, a_in, b_in, a_sum, b_sum, a_last, b_last, flat), sems[8:16], started
     )
@@ -359,7 +363,7 @@
         return inner
 
     row = lax.broadcasted_iota(jnp.int32, (ROWS, CHANNELS), 0)
-    valid = lax.rem(row, PITCH) < SIDE
+    valid = (lax.rem(row, PITCH) < SIDE) & (row < PITCH * SIDE)
 
     def whole(h, item):
         return w[h, item].reshape(CHANNELS, 128)
@@ -373,35 +377,47 @@
     def head(h):
         return jnp.concatenate([whole(h, HEAD + k) for k in range(5)], axis=1)
 
-    def conv(field, kernel, flip):
-        taps = [8 - t if flip else t for t in range(9)]
-        lhs = jnp.concatenate(
-            [field[t % 3, PITCH * (t // 3) : PITCH * (t // 3) + ROWS] for t in range(9)], axis=1
-        )
-        return lhs, [kernel(t) for t in taps]
+    def halves(lhs, rhs):
+        cut = ROWS // 2
+        return jnp.concatenate([dot(lhs[:cut], rhs), dot(lhs[cut:], rhs)], axis=0)
 
     @phase
-    def conv_plain(field, kernel, flip):
-        lhs, parts = conv(field, kernel, flip)
-        rhs = jnp.concatenate(parts, axis=0)
-        return jnp.concatenate([dot(lhs[: ROWS // 2], rhs), dot(lhs[ROWS // 2 :], rhs)], axis=0)
+    def transposes(dest, kernel, flip):
+        for tap in range(9):
+            turn = kernel(8 - tap if flip else tap).astype(F32).T
+            dest[CHANNELS * tap : CHANNELS * tap + CHANNELS, :] = turn.astype(BF16)
+
+    def taps_of(field):
+        return jnp.concatenate([field[t] for t in range(9)], axis=1)
 
     @phase
-    def conv_swapped(field, kernel, flip):
-        lhs, parts = conv(field, kernel, flip)
-        rhs = jnp.concatenate(parts, axis=1)
-        return jnp.concatenate([dot(lhs[: ROWS // 2], rhs, NT), dot(lhs[ROWS // 2 :], rhs, NT)], axis=0)
+    def conv_first(field):
+        return halves(taps_of(field), jnp.concatenate([first(t) for t in range(9)], axis=0))
+
+    @phase
+    def conv_second(field):
+        return halves(taps_of(field), second_t[...])
+
+    @phase
+    def back_second(field):
+        return halves(taps_of(field), jnp.concatenate([second(8 - t) for t in range(9)], axis=0))
+
+    @phase
+    def back_first(field):
+        return halves(taps_of(field), first_t[...])
 
     @phase
     def spread(value, dest):
-        dest[1, PITCH : PITCH + ROWS] = value.astype(BF16)
-        dest[0, PITCH : PITCH + ROWS] = pltpu.roll(value, 1, 0).astype(BF16)
-        dest[2, PITCH : PITCH + ROWS] = pltpu.roll(value, ROWS - 1, 0).astype(BF16)
+        for h in range(2):
+            lanes = slice(128 * h, 128 * h + 128)
+            slabs[h, GUARD : GUARD + ROWS, :] = value[:, lanes]
+            for t in range(9):
+                start = GUARD + SHIFTS[t]
+                dest[t, :, lanes] = slabs[h, start : start + ROWS, :].astype(BF16)
 
     @phase
     def turned(value):
-        tall = jnp.concatenate([value, jnp.zeros((TALL - ROWS, CHANNELS), F32)], axis=0)
-        return tall.T.astype(BF16)
+        return value.T.astype(BF16)
 
     def total(value):
         return jnp.sum(jnp.sum(value, axis=0, keepdims=True), axis=1, keepdims=True)
@@ -409,24 +425,20 @@
     def store(h, item, value):
         g[h, item] = value.astype(BF16).reshape(4, 4, 16, 128)
 
-    for field in (xs, hs, bs, zs):
-        for k in range(2):
-            for b in range(3):
-                field[k, b, 0:PITCH] = jnp.zeros((PITCH, CHANNELS), BF16)
-                field[k, b, PITCH + ROWS : DEPTH] = jnp.zeros((DEPTH - PITCH - ROWS, CHANNELS), BF16)
+    for h in range(2):
+        slabs[h, 0:GUARD, :] = jnp.zeros((GUARD, 128), F32)
+        slabs[h, GUARD + ROWS :, :] = jnp.zeros((GUARD, 128), F32)
     flat[16 * FIRST : 16 * FIRST + 32, :] = jnp.zeros((32, 128), F32)
 
     state[...] = jnp.zeros((ROWS, CHANNELS), F32)
-    loads[4].wait()
-
-    def place(line, carry):
-        cells = hidden_v[line].astype(F32)
-        mine = jnp.where(c == 0, cells[:, 0, :], cells[:, 1, :])
-        state[pl.ds(pl.multiple_of(PITCH * line, PITCH), SIDE), :] = mine
-        return carry
+    for load in loads[4:8]:
+        load.wait()
 
     with jax.named_scope("place"):
-        lax.fori_loop(0, SIDE, place, 0)
+        for line in range(SIDE):
+            cells = hidden_v[line].astype(F32)
+            mine = jnp.where(c == 0, cells[:, 0, :], cells[:, 1, :])
+            state[PITCH * line : PITCH * line + SIDE, :] = mine
     lane = lax.broadcasted_iota(jnp.int32, (CHANNELS, CHANNELS), 1)
     natural = 64 * (lane // 64) + 8 * (lane % 8) + 2 * ((lane // 16) % 4) + (lane // 8) % 2
     source = lax.broadcasted_iota(jnp.int32, (CHANNELS, CHANNELS), 0)
@@ -438,12 +450,14 @@
     gather.own_sends(2)
     gather.unpack(0)
     gather.near_sends(1)
+    gather.own_sends(1)
     gather.near_sends(0)
     gather.far_sends(2)
-    for chunk in (1, 0):
-        gather.own_sends(chunk)
-        gather.far_sends(chunk)
-    gather.finish(2)
+    gather.far_sends(1)
+    gather.own_sends(0)
+    gather.far_sends(0)
+    gather.cross(2)
+    gather.join(2)
 
     ones = jnp.ones((16, 128), BF16)
     pick = lax.broadcasted_iota(jnp.int32, (16, 128), 1) == 0
@@ -459,14 +473,20 @@
         added = jnp.where(row == spot, embed[0], 0.0) + jnp.where(passed, 1.0, 0.0) * embed[1]
         now = jnp.where(valid, state[...] + added, 0.0)
         mixed[...] = now
+        if k == 1:
+            gather.cross(0)
         spread(now, xs.at[k])
-        xt[:, TALL * k : TALL * k + TALL] = turned(now)
-        value = SCALE * conv_plain(xs.at[k], first, False)
+        value = SCALE * conv_first(xs.at[k])
         pre[k] = value
         spread(jnp.where(valid, value * jax.nn.sigmoid(value), 0.0), hs.at[k])
         if k == 0:
-            gather.finish(1)
-        branch = conv_swapped(hs.at[k], second, False)
+            gather.cross(1)
+        xt[:, ROWS * k : ROWS * k + ROWS] = turned(mixed[...])
+        if k == 0:
+            transposes(first_t, first, True)
+            gather.join(1)
+            transposes(second_t, second, False)
+        branch = conv_second(hs.at[k])
         value = jnp.where(valid, mixed[...] + SCALE * branch, 0.0)
         summed[k] = value
         factor = lax.rsqrt(total(value * value) / (CELLS * CHANNELS) + eps_norm)
@@ -476,7 +496,7 @@
         own_row = lax.broadcasted_iota(jnp.int32, (16, CHANNELS), 0) == k
         pooled_rows = jnp.where(own_row, pooled, pooled_rows)
         kept.append((spot, passed, factor))
-    gather.finish(0)
+    gather.join(0)
 
     bucket = lax.broadcasted_iota(jnp.int32, (16, 640), 1)
     top_row = lax.broadcasted_iota(jnp.int32, (16, 640), 0) == 0
@@ -501,8 +521,7 @@
         scatter.to_partner(piece)
 
     def window(field, tap):
-        start = PITCH * (tap // 3)
-        return jnp.concatenate([field[k, tap % 3, start : start + TALL] for k in range(2)], axis=0)
+        return jnp.concatenate([field[k, tap] for k in range(2)], axis=0)
 
     def second_taps(*taps):
         with jax.named_scope("second_taps"):
@@ -530,7 +549,7 @@
         summed_grad = factor * grad - factor * factor * factor * value * slope
         saved[...] = summed_grad
         spread(summed_grad, bs.at[k])
-        bt[:, TALL * k : TALL * k + TALL] = turned(summed_grad)
+        bt[:, ROWS * k : ROWS * k + ROWS] = turned(summed_grad)
         if k == 0:
             second_taps(0, 1, 2)
             scatter.to_partner(2)
@@ -538,35 +557,30 @@
             scatter.to_partner(3)
             second_taps(5, 6)
             scatter.to_partner(4)
-            scatter.near_sends(2)
             second_taps(7, 8)
             scatter.to_partner(5)
+            scatter.near_sends(2)
             scatter.near_sends(3)
-        hidden_grad = SCALE * conv_plain(bs.at[k], second, True)
-        for piece in ((4, 5), (0, 1))[k]:
-            scatter.near_sends(piece)
+        hidden_grad = SCALE * back_second(bs.at[k])
+        if k == 0:
+            scatter.near_sends(4)
         value = pre[k]
         sig = jax.nn.sigmoid(value)
         inner = hidden_grad * (sig * (1.0 + value * (1.0 - sig)))
         spread(jnp.where(valid, inner, 0.0), zs.at[k])
+        for piece in ((5,), (0, 1))[k]:
+            scatter.near_sends(piece)
         if k == 0:
             first_taps(0, 1)
             scatter.to_partner(6)
             first_taps(2, 3)
             scatter.to_partner(7)
-            first_taps(4, 5)
-            scatter.to_partner(8)
+            for piece in (0, 1):
+                scatter.far_sends(piece)
+        carry = saved[...] + SCALE * back_first(zs.at[k])
+        if k == 0:
             scatter.near_sends(6)
-            first_taps(6, 7)
-            scatter.to_partner(9)
             scatter.near_sends(7)
-            first_taps(8)
-            scatter.to_partner(10)
-            scatter.near_sends(8)
-            scatter.near_sends(9)
-        carry = saved[...] + SCALE * conv_swapped(zs.at[k], first, True)
-        if k == 0:
-            scatter.near_sends(10)
         carry = jnp.where(valid, carry, 0.0)
         saved[...] = carry
         embed_grad[0] = embed_grad[0] + jnp.sum(jnp.where(row == spot, carry, 0.0), axis=0, keepdims=True)
@@ -577,15 +591,24 @@
         top = lax.broadcasted_iota(jnp.int32, (16, 128), 0) == 0
         store(e, EMBED, dot(lines, jnp.where(top, ones, jnp.zeros_like(ones)), TN))
     scatter.to_partner(11)
-    for piece in (0, 1, 2, 3):
+    first_taps(4, 5)
+    scatter.to_partner(8)
+    first_taps(6, 7)
+    scatter.to_partner(9)
+    first_taps(8)
+    scatter.to_partner(10)
+    for piece in (8, 11, 9, 10):
+        scatter.near_sends(piece)
+    for piece in (2, 3, 4, 5, 6, 7):
         scatter.far_sends(piece)
-    scatter.near_sends(11)
-    for piece in (4, 5, 6, 7, 8, 9, 10):
+    for copy in sent:
+        copy.wait_send()
+    for piece in (8, 9, 11):
         scatter.far_sends(piece)
-    for piece in (0, 1, 2, 3):
+    for piece in (0, 1):
         scatter.settle(piece)
-    scatter.far_sends(11)
-    for piece in (4, 5):
+    scatter.far_sends(10)
+    for piece in (2, 3, 4, 5):
         scatter.settle(piece)
     scatter.along_z(0, 0, early_out, early)
     for piece in (6, 7, 8, 9, 10, 11):
@@ -600,11 +623,10 @@
 
 def window_grads(moves, values, rewards, hidden_state, params):
     vmem = pl.BlockSpec(memory_space=pltpu.VMEM)
-    smem = pl.BlockSpec(memory_space=pltpu.SMEM)
     hbm = pl.BlockSpec(memory_space=pltpu.HBM)
     dma = pltpu.SemaphoreType.DMA
-    copies = pltpu.VMEM((2, 3, DEPTH, CHANNELS), BF16)
-    turned = pltpu.VMEM((CHANNELS, 2 * TALL), BF16)
+    copies = pltpu.VMEM((2, 9, ROWS, CHANNELS), BF16)
+    turned = pltpu.VMEM((CHANNELS, 2 * ROWS), BF16)
     field = pltpu.VMEM((ROWS, CHANNELS), F32)
     fields = pltpu.VMEM((2, ROWS, CHANNELS), F32)
     board = pltpu.VMEM((ITEMS, 4, 4, 16, 128), BF16)
@@ -613,7 +635,7 @@
     return pl.pallas_call(
         window_kernel,
         out_shape=[jax.ShapeDtypeStruct(early, BF16), jax.ShapeDtypeStruct(late, BF16)],
-        in_specs=[smem] * 3 + [hbm] * 5,
+        in_specs=[hbm] * 8,
         out_specs=[vmem, vmem],
         scratch_shapes=[pltpu.VMEM(p.shape, F32) for p in params]
         + [
@@ -645,7 +667,13 @@
             fields,
             fields,
             field,
-            dma((5,)),
+            pltpu.VMEM((2, ROWS + 2 * GUARD, 128), F32),
+            pltpu.VMEM((9 * CHANNELS, CHANNELS), BF16),
+            pltpu.VMEM((9 * CHANNELS, CHANNELS), BF16),
+            pltpu.SMEM((2, 2), jnp.int32),
+            pltpu.SMEM((2, 2), jnp.int32),
+            pltpu.SMEM((2, 2), jnp.int32),
+            dma((8,)),
         ]
         + [
             dma(shape)

time: 66.2 us -> 62.4 us (0.943)
  Pallas kernels: 65.4 us -> 61.4 us
    pallas_call x1, Pallas kernels: 63.6 us -> 59.6 us  [window_grads(): pl.pallas_call(window_kernel, out_shape=[jax.ShapeDtypeStruct(early, BF16...]
where the time goes in v3:
time: 62.4 us; the launch traced here: 62 us
  Pallas kernels  61.4 us (98%)
  between operations  0.65 us (1%)
    pallas_call x1, Pallas kernels, window_grads(): pl.pallas_call(window_kernel, out_shape=[jax.ShapeDtypeStruct(early, BF16...  59.6 us
    pallas_call x1, Pallas kernels, updates(): pl.pallas_call(adam_kernel, out_shape=shapes * 4, in_specs=[pl.BlockSpec(...  1.79 us

profile of v3, /device:TPU:2, one launch (start us, length us, event | category | flops | bytes accessed | tf_op | source)
XLA Modules:
  0.0 62.0 jit_solution(10049802327933310449)
XLA Ops:
  0.6 59.6 %window.1 = (bf16[8,32,128]{2,1,0:T(8,128)(2,1)}, bf16[8,24,128]{2,1,0:T(8,128)(2,1)}) custom-call(s32[2,2]{1,0:T(2,128)} %moves_in.1, s32[2,2]{1,0:T(2,128)} %values_in.1, s32[2,2]{1,0:T(2,128)} %rewards_in.1, bf16[19,19,2,256]{3,2,1,0:T(2,128)(2,1)} %bitcast.1, f32[3,3,2,128]{3,2,1,0:T(2,128)} %refs_2_.1, f32[3,3,2,128]{3,2,1,0:T(2,128)} %refs_3_.1, ...), custom_call_target="tpu_custom_call" | custom-call | tf_op jit(solution)/shard_map/window/pallas_call | solution.py:635
  60.2 1.8 %adam.1 = (f32[3,3,2,128]{3,2,1,0:T(2,128)}, f32[3,3,2,128]{3,2,1,0:T(2,128)}, f32[1,2,601]{2,1,0:T(2,128)}, f32[1,2]{1,0:T(1,128)}, f32[3,3,2,128]{3,2,1,0:T(2,...) custom-call(bf16[8,32,128]{2,1,0:T(8,128)(2,1)} %get-tuple-element.3, ...), custom_call_target="tpu_custom_call" | custom-call | tf_op jit(solution)/shard_map/adam/pallas_call | solution.py:743

commit v4 on v3

--- a/solution.py
+++ b/solution.py
@@ -18,13 +18,14 @@
 ROWS = 384
 GUARD = 24
 SHIFTS = tuple(PITCH * (t // 3 - 1) + t % 3 - 1 for t in range(9))
-ITEMS = 24
-HEAD, SECOND, FIRST, EMBED = 0, 5, 14, 23
-CHUNKS = (((0, 2), (2, 3)), ((5, 5), (10, 4)), ((14, 5), (19, 5)))
+ITEMS = 23
+HEAD, SECOND, FIRST, MIX = 0, 4, 13, 22
+SPLIT = 11
+CHUNKS = ({0: (0, 2), 1: (2, 2)}, {0: (4, 5), 1: (9, 4)}, {0: (13, 4), 1: (17, 5)}, {0: (22, 1)})
 PIECES = (
-    (0, 0, 2, 0), (1, 2, 3, 0),
-    (0, 5, 3, 2), (1, 8, 2, 3), (0, 10, 2, 5), (1, 12, 2, 5),
-    (0, 14, 2, 7), (1, 16, 2, 7), (0, 18, 2, 9), (1, 20, 2, 9), (0, 22, 1, 11), (1, 23, 1, 11),
+    (0, 0, 2, 0), (1, 2, 2, 0),
+    (0, 4, 1, 2), (1, 5, 2, 2), (0, 7, 2, 3), (1, 9, 2, 4), (0, 11, 2, 5),
+    (1, 13, 2, 6), (0, 15, 2, 7), (1, 17, 2, 8), (0, 19, 2, 9), (1, 21, 1, 10), (0, 22, 1, 11),
 )
 HALVES = (("dp_2", "dp_0"), ("dp_0", "dp_2"))
 ORDER = (1, 3, 2)
@@ -86,6 +87,10 @@
     remote(ref, ref, send, recv, peer).wait_recv()
 
 
+def halves_of(chunk):
+    return [(half, *HALVES[half]) for half in CHUNKS[chunk]]
+
+
 class Gather:
     def __init__(self, seat, w, stage, wide, sems, started):
         self.y, self.z, self.x, self.c = seat
@@ -143,16 +148,17 @@
 
     @scoped
     def near_sends(self, chunk):
-        for half, (near, far) in enumerate(HALVES):
+        for half, near, far in halves_of(chunk):
             start, count = CHUNKS[chunk][half]
             for item in range(start, start + count):
-                group, line = item // 12, 2 * (item % 12)
+                group = int(item >= SPLIT)
+                line = 2 * (item - SPLIT * group)
                 slab = self.wide.at[group]
                 low = slab[pl.ds(line, 8, stride=24), :]
                 high = slab[pl.ds(line + 1, 8, stride=24), :]
                 self.w[self.c, item, self.y, self.x] = jnp.concatenate([low, high], axis=0).astype(BF16)
         for step in ORDER:
-            for half, (near, far) in enumerate(HALVES):
+            for half, near, far in halves_of(chunk):
                 at = self.here[near]
                 ref = self.tile(chunk, half, at, self.here[far])
                 self.launch(
@@ -163,7 +169,7 @@
                 )
 
     def own_sends(self, chunk):
-        for half, (near, far) in enumerate(HALVES):
+        for half, near, far in halves_of(chunk):
             self.to_far(chunk, half, 0, self.here[near])
 
     def to_partner(self, chunk, half, turn, ref):
@@ -173,18 +179,18 @@
     @scoped
     def far_sends(self, chunk):
         for step in ORDER:
-            for half, (near, far) in enumerate(HALVES):
+            for half, near, far in halves_of(chunk):
                 peer = lax.rem(self.here[near] + step, 4)
                 ref = self.tile(chunk, half, peer, self.here[far])
                 arrived(ref, self.p_recv.at[chunk, half, peer], self.p_send.at[chunk, half, 0], {near: peer})
                 self.to_far(chunk, half, step, peer)
-        for half, (near, far) in enumerate(HALVES):
+        for half, near, far in halves_of(chunk):
             self.to_partner(chunk, half, 0, self.slab(chunk, half, self.here[far], self.c))
 
     @scoped
     def cross(self, chunk):
         for step in ORDER:
-            for half, (near, far) in enumerate(HALVES):
+            for half, near, far in halves_of(chunk):
                 peer = lax.rem(self.here[far] + step, 4)
                 ref = self.slab(chunk, half, peer, self.c)
                 arrived(ref, self.q_recv.at[chunk, half, peer], self.q_send.at[chunk, half, 0, 0], {far: peer})
@@ -192,7 +198,7 @@
 
     @scoped
     def join(self, chunk):
-        for half, (near, far) in enumerate(HALVES):
+        for half, near, far in halves_of(chunk):
             for turn in range(4):
                 ref = self.slab(chunk, half, lax.rem(self.here[far] + turn, 4), 1 - self.c)
                 sems = self.m_recv.at[chunk, half, turn], self.m_send.at[chunk, half, turn]
@@ -334,7 +340,7 @@
     scatter = Scatter(
         seat, g, (inbox, sums, a_in, b_in, a_sum, b_sum, a_last, b_last, flat), sems[8:16], started
     )
-    rows[2 * HEAD : 2 * SECOND, :] = jnp.zeros((10, 128), F32)
+    rows[2 * MIX : 2 * MIX + 4, :] = jnp.zeros((4, 128), F32)
     for load in loads[0:4]:
         load.wait()
     for tap in range(9):
@@ -344,13 +350,13 @@
         rows[at : at + 2, :] = first_v[tap // 3, tap % 3]
     for block in range(5):
         width = min(128, BUCKETS - 128 * block)
-        at = 2 * (HEAD + block)
+        at = 2 * (HEAD + block if block < 4 else MIX)
         rows[at : at + 2, 0:width] = head_v[0, :, 128 * block : 128 * block + width]
     for r in range(2):
-        at = 2 * EMBED + r
-        rows[at : at + 1, :] = jnp.broadcast_to(embed_v[:, r : r + 1], (1, 128))
-    for group in range(2):
-        stage[group, z] = rows[24 * group : 24 * group + 24, :].astype(BF16)
+        at = 2 * MIX + r
+        rows[at : at + 1, 127:128] = embed_v[:, r : r + 1]
+    stage[0, z] = rows[0:24, :].astype(BF16)
+    stage[1, z] = rows[2 * SPLIT : 2 * SPLIT + 24, :].astype(BF16)
     with jax.named_scope("barrier"):
         pl.semaphore_wait(barrier, 14)
     gather.along_z()
@@ -375,7 +381,9 @@
         return jnp.concatenate([whole(0, SECOND + tap), whole(1, SECOND + tap)], axis=1)
 
     def head(h):
-        return jnp.concatenate([whole(h, HEAD + k) for k in range(5)], axis=1)
+        last = whole(h, MIX)
+        last = jnp.where(lax.broadcasted_iota(jnp.int32, last.shape, 1) < BUCKETS - 512, last, jnp.zeros_like(last))
+        return jnp.concatenate([whole(h, HEAD + k) for k in range(4)] + [last], axis=1)
 
     def halves(lhs, rhs):
         cut = ROWS // 2
@@ -428,7 +436,7 @@
     for h in range(2):
         slabs[h, 0:GUARD, :] = jnp.zeros((GUARD, 128), F32)
         slabs[h, GUARD + ROWS :, :] = jnp.zeros((GUARD, 128), F32)
-    flat[16 * FIRST : 16 * FIRST + 32, :] = jnp.zeros((32, 128), F32)
+    flat[16 * FIRST : 16 * FIRST + 48, :] = jnp.zeros((48, 128), F32)
 
     state[...] = jnp.zeros((ROWS, CHANNELS), F32)
     for load in loads[4:8]:
@@ -446,23 +454,25 @@
     state[...] = dot(state[...].astype(BF16), permute)
 
     gather.unpack(1)
-    gather.near_sends(2)
-    gather.own_sends(2)
+    for chunk in (3, 2):
+        gather.near_sends(chunk)
+        gather.own_sends(chunk)
     gather.unpack(0)
-    gather.near_sends(1)
-    gather.own_sends(1)
-    gather.near_sends(0)
-    gather.far_sends(2)
-    gather.far_sends(1)
-    gather.own_sends(0)
-    gather.far_sends(0)
+    for chunk in (1, 0):
+        gather.near_sends(chunk)
+    for chunk in (3, 2):
+        gather.far_sends(chunk)
+    for chunk in (1, 0):
+        gather.own_sends(chunk)
+        gather.far_sends(chunk)
+    gather.cross(3)
     gather.cross(2)
-    gather.join(2)
+    gather.join(3)
 
     ones = jnp.ones((16, 128), BF16)
-    pick = lax.broadcasted_iota(jnp.int32, (16, 128), 1) == 0
+    pick = lax.broadcasted_iota(jnp.int32, (16, 128), 1) == 127
     pick = jnp.where(pick, ones, jnp.zeros_like(ones))
-    embed = [dot(pick, whole(e, EMBED), NT)[0:1, :] for e in range(2)]
+    embed = [dot(pick, whole(e, MIX), NT)[0:1, :] for e in range(2)]
 
     kept = []
     pooled_rows = jnp.zeros((16, CHANNELS), F32)
@@ -476,13 +486,14 @@
         if k == 1:
             gather.cross(0)
         spread(now, xs.at[k])
+        if k == 0:
+            gather.join(2)
         value = SCALE * conv_first(xs.at[k])
         pre[k] = value
         spread(jnp.where(valid, value * jax.nn.sigmoid(value), 0.0), hs.at[k])
         if k == 0:
             gather.cross(1)
-        xt[:, ROWS * k : ROWS * k + ROWS] = turned(mixed[...])
-        if k == 0:
+            xt[:, 0:ROWS] = turned(mixed[...])
             transposes(first_t, first, True)
             gather.join(1)
             transposes(second_t, second, False)
@@ -513,10 +524,12 @@
         logit = jnp.where(bucket < BUCKETS, logit, 0.0).astype(BF16)
         pooled_grads = pooled_grads + dot(logit, head(h), NT)
         logits.append(logit)
+    mixed_grads = []
     for h in range(2):
         grad = head_scale * dot(pooled, logits[h], TN)
-        for block in range(5):
+        for block in range(4):
             store(h, HEAD + block, grad[:, 128 * block : 128 * block + 128])
+        mixed_grads.append(grad[:, 512:640])
     for piece in (0, 1):
         scatter.to_partner(piece)
 
@@ -551,36 +564,42 @@
         spread(summed_grad, bs.at[k])
         bt[:, ROWS * k : ROWS * k + ROWS] = turned(summed_grad)
         if k == 0:
-            second_taps(0, 1, 2)
+            second_taps(0)
             scatter.to_partner(2)
+            second_taps(1, 2)
+            scatter.to_partner(3)
             second_taps(3, 4)
-            scatter.to_partner(3)
+            scatter.to_partner(4)
+            xt[:, ROWS : 2 * ROWS] = turned(mixed[...])
+            scatter.near_sends(2)
             second_taps(5, 6)
-            scatter.to_partner(4)
+            scatter.to_partner(5)
+            scatter.near_sends(3)
             second_taps(7, 8)
-            scatter.to_partner(5)
-            scatter.near_sends(2)
-            scatter.near_sends(3)
+            scatter.to_partner(6)
+            scatter.near_sends(4)
         hidden_grad = SCALE * back_second(bs.at[k])
         if k == 0:
-            scatter.near_sends(4)
+            scatter.near_sends(5)
         value = pre[k]
         sig = jax.nn.sigmoid(value)
         inner = hidden_grad * (sig * (1.0 + value * (1.0 - sig)))
         spread(jnp.where(valid, inner, 0.0), zs.at[k])
-        for piece in ((5,), (0, 1))[k]:
-            scatter.near_sends(piece)
         if k == 0:
+            scatter.near_sends(6)
             first_taps(0, 1)
-            scatter.to_partner(6)
+            scatter.to_partner(7)
             first_taps(2, 3)
-            scatter.to_partner(7)
+            scatter.to_partner(8)
             for piece in (0, 1):
                 scatter.far_sends(piece)
         carry = saved[...] + SCALE * back_first(zs.at[k])
         if k == 0:
-            scatter.near_sends(6)
             scatter.near_sends(7)
+            scatter.near_sends(8)
+        else:
+            scatter.near_sends(0)
+            scatter.near_sends(1)
         carry = jnp.where(valid, carry, 0.0)
         saved[...] = carry
         embed_grad[0] = embed_grad[0] + jnp.sum(jnp.where(row == spot, carry, 0.0), axis=0, keepdims=True)
@@ -588,32 +607,33 @@
 
     for e in range(2):
         lines = jnp.broadcast_to(embed_grad[e], (16, CHANNELS)).astype(BF16)
-        top = lax.broadcasted_iota(jnp.int32, (16, 128), 0) == 0
-        store(e, EMBED, dot(lines, jnp.where(top, ones, jnp.zeros_like(ones)), TN))
+        corner = lax.broadcasted_iota(jnp.int32, (16, 128), 0) * 128 + lax.broadcasted_iota(jnp.int32, (16, 128), 1)
+        corner = jnp.where(corner == 127, ones, jnp.zeros_like(ones))
+        store(e, MIX, mixed_grads[e] + dot(lines, corner, TN))
+    scatter.to_partner(12)
+    first_taps(4, 5)
+    scatter.to_partner(9)
+    first_taps(6, 7)
+    scatter.to_partner(10)
+    first_taps(8)
     scatter.to_partner(11)
-    first_taps(4, 5)
-    scatter.to_partner(8)
-    first_taps(6, 7)
-    scatter.to_partner(9)
-    first_taps(8)
-    scatter.to_partner(10)
-    for piece in (8, 11, 9, 10):
+    for piece in (9, 12, 10, 11):
         scatter.near_sends(piece)
-    for piece in (2, 3, 4, 5, 6, 7):
+    for piece in (2, 3, 4, 5, 6, 7, 8):
         scatter.far_sends(piece)
     for copy in sent:
         copy.wait_send()
-    for piece in (8, 9, 11):
+    for piece in (9, 12, 10):
         scatter.far_sends(piece)
     for piece in (0, 1):
         scatter.settle(piece)
-    scatter.far_sends(10)
-    for piece in (2, 3, 4, 5):
+    scatter.far_sends(11)
+    for piece in (2, 3, 4, 5, 6):
         scatter.settle(piece)
     scatter.along_z(0, 0, early_out, early)
-    for piece in (6, 7, 8, 9, 10, 11):
+    for piece in (7, 8, 9, 12, 10, 11):
         scatter.settle(piece)
-    scatter.along_z(1, 12, late_out, late)
+    scatter.along_z(1, SPLIT, late_out, late)
     scatter.collect(0, early)
     scatter.collect(1, late)
     with jax.named_scope("drain"):
@@ -678,8 +698,8 @@
         + [
             dma(shape)
             for shape in (
-                (2, 8), (2, 8), (3, 2, 4), (3, 2, 4), (3, 2, 4, 4), (3, 2, 4), (3, 2, 4), (3, 2, 4),
-                (12,), (12,), (12, 4), (12, 4), (12, 4), (12, 4), (2, 8), (2, 8),
+                (2, 8), (2, 8), (4, 2, 4), (4, 2, 4), (4, 2, 4, 4), (4, 2, 4), (4, 2, 4), (4, 2, 4),
+                (13,), (13,), (13, 4), (13, 4), (13, 4), (13, 4), (2, 8), (2, 8),
             )
         ],
         compiler_params=pltpu.CompilerParams(
@@ -716,7 +736,7 @@
     def owned(item):
         if item < FIRST:
             return totals[0][2 * item : 2 * item + 2]
-        return totals[1][2 * (item - 12) : 2 * (item - 12) + 2]
+        return totals[1][2 * (item - SPLIT) : 2 * (item - SPLIT) + 2]
 
     for which in range(2):
         for tap in range(9):
@@ -725,12 +745,12 @@
             results = adam(params[which][a, b], grad, means[which][a, b], squares[which][a, b])
             for ref, result in zip((new, mean_new, square_new, grads), results):
                 ref[which][a, b] = result
-    head = jnp.concatenate([owned(HEAD + k) for k in range(5)], axis=1)[:, 0:BUCKETS]
+    head = jnp.concatenate([owned(HEAD + k) for k in range(4)] + [owned(MIX)], axis=1)[:, 0:BUCKETS]
     results = adam(params[2][0], head, means[2][0], squares[2][0])
     for ref, result in zip((new, mean_new, square_new, grads), results):
         ref[2][0] = result
-    embed = owned(EMBED)
-    embed = jnp.concatenate([embed[0:1, 0:1], embed[1:2, 0:1]], axis=1)
+    embed = owned(MIX)
+    embed = jnp.concatenate([embed[0:1, 127:128], embed[1:2, 127:128]], axis=1)
     results = adam(params[3][...], embed, means[3][...], squares[3][...])
     for ref, result in zip((new, mean_new, square_new, grads), results):
         ref[3][...] = result

time: 62.4 us -> 62.3 us (level)
  no operation moved by 1% of the time
where the time goes in v4:
time: 62.3 us; the launch traced here: 62 us
  Pallas kernels  61.2 us (98%)
  between operations  0.82 us (1%)
    pallas_call x1, Pallas kernels, window_grads(): pl.pallas_call(window_kernel, out_shape=[jax.ShapeDtypeStruct(early, BF16...  59.4 us
    pallas_call x1, Pallas kernels, updates(): pl.pallas_call(adam_kernel, out_shape=shapes * 4, in_specs=[pl.BlockSpec(...  1.79 us

profile of v4, /device:TPU:2, one launch (start us, length us, event | category | flops | bytes accessed | tf_op | source)
XLA Modules:
  0.0 62.0 jit_solution(2338432572350733972)
XLA Ops:
  0.6 59.4 %window.1 = (bf16[8,32,128]{2,1,0:T(8,128)(2,1)}, bf16[8,24,128]{2,1,0:T(8,128)(2,1)}) custom-call(s32[2,2]{1,0:T(2,128)} %moves_in.1, s32[2,2]{1,0:T(2,128)} %values_in.1, s32[2,2]{1,0:T(2,128)} %rewards_in.1, bf16[19,19,2,256]{3,2,1,0:T(2,128)(2,1)} %bitcast.1, f32[3,3,2,128]{3,2,1,0:T(2,128)} %refs_2_.1, f32[3,3,2,128]{3,2,1,0:T(2,128)} %refs_3_.1, ...), custom_call_target="tpu_custom_call" | custom-call | tf_op jit(solution)/shard_map/window/pallas_call | solution.py:655
  60.1 1.8 %adam.1 = (f32[3,3,2,128]{3,2,1,0:T(2,128)}, f32[3,3,2,128]{3,2,1,0:T(2,128)}, f32[1,2,601]{2,1,0:T(2,128)}, f32[1,2]{1,0:T(1,128)}, f32[3,3,2,128]{3,2,1,0:T(2,...) custom-call(bf16[8,32,128]{2,1,0:T(8,128)(2,1)} %get-tuple-element.3, ...), custom_call_target="tpu_custom_call" | custom-call | tf_op jit(solution)/shard_map/adam/pallas_call | solution.py:763

commit v5 on v4

--- a/solution.py
+++ b/solution.py
@@ -324,7 +324,7 @@
     moves_in, values_in, rewards_in, hidden_in, first_in, second_in, head_in, embed_in, early, late,
     first_v, second_v, head_v, embed_v, hidden_v, rows, stage, wide, w, g,
     inbox, sums, a_in, b_in, a_sum, b_sum, a_last, b_last, flat, early_out, late_out,
-    xs, hs, bs, zs, xt, bt, state, mixed, pre, summed, saved, slabs, first_t, second_t, moves, values, rewards, local_sem, *sems,
+    xs, hs, bs, zs, xt, bt, state, mixed, pre, summed, saved, first_t, second_t, moves, values, rewards, local_sem, *sems,
 ):
     seat = y, z, x, c = seats()
     barrier = greet_all(y, z, x, c)
@@ -385,6 +385,10 @@
         last = jnp.where(lax.broadcasted_iota(jnp.int32, last.shape, 1) < BUCKETS - 512, last, jnp.zeros_like(last))
         return jnp.concatenate([whole(h, HEAD + k) for k in range(4)] + [last], axis=1)
 
+    def shifted(field, tap):
+        start = GUARD + SHIFTS[tap]
+        return jnp.concatenate([field[h, start : start + ROWS, :].astype(BF16) for h in range(2)], axis=1)
+
     def halves(lhs, rhs):
         cut = ROWS // 2
         return jnp.concatenate([dot(lhs[:cut], rhs), dot(lhs[cut:], rhs)], axis=0)
@@ -396,7 +400,7 @@
             dest[CHANNELS * tap : CHANNELS * tap + CHANNELS, :] = turn.astype(BF16)
 
     def taps_of(field):
-        return jnp.concatenate([field[t] for t in range(9)], axis=1)
+        return jnp.concatenate([shifted(field, t) for t in range(9)], axis=1)
 
     @phase
     def conv_first(field):
@@ -417,11 +421,7 @@
     @phase
     def spread(value, dest):
         for h in range(2):
-            lanes = slice(128 * h, 128 * h + 128)
-            slabs[h, GUARD : GUARD + ROWS, :] = value[:, lanes]
-            for t in range(9):
-                start = GUARD + SHIFTS[t]
-                dest[t, :, lanes] = slabs[h, start : start + ROWS, :].astype(BF16)
+            dest[h, GUARD : GUARD + ROWS, :] = value[:, 128 * h : 128 * h + 128]
 
     @phase
     def turned(value):
@@ -433,9 +433,11 @@
     def store(h, item, value):
         g[h, item] = value.astype(BF16).reshape(4, 4, 16, 128)
 
-    for h in range(2):
-        slabs[h, 0:GUARD, :] = jnp.zeros((GUARD, 128), F32)
-        slabs[h, GUARD + ROWS :, :] = jnp.zeros((GUARD, 128), F32)
+    for field in (xs, hs, bs, zs):
+        for k in range(2):
+            for h in range(2):
+                field[k, h, 0:GUARD, :] = jnp.zeros((GUARD, 128), F32)
+                field[k, h, GUARD + ROWS :, :] = jnp.zeros((GUARD, 128), F32)
     flat[16 * FIRST : 16 * FIRST + 48, :] = jnp.zeros((48, 128), F32)
 
     state[...] = jnp.zeros((ROWS, CHANNELS), F32)
@@ -534,7 +536,7 @@
         scatter.to_partner(piece)
 
     def window(field, tap):
-        return jnp.concatenate([field[k, tap] for k in range(2)], axis=0)
+        return jnp.concatenate([shifted(field.at[k], tap) for k in range(2)], axis=0)
 
     def second_taps(*taps):
         with jax.named_scope("second_taps"):
@@ -645,7 +647,7 @@
     vmem = pl.BlockSpec(memory_space=pltpu.VMEM)
     hbm = pl.BlockSpec(memory_space=pltpu.HBM)
     dma = pltpu.SemaphoreType.DMA
-    copies = pltpu.VMEM((2, 9, ROWS, CHANNELS), BF16)
+    copies = pltpu.VMEM((2, 2, ROWS + 2 * GUARD, 128), F32)
     turned = pltpu.VMEM((CHANNELS, 2 * ROWS), BF16)
     field = pltpu.VMEM((ROWS, CHANNELS), F32)
     fields = pltpu.VMEM((2, ROWS, CHANNELS), F32)
@@ -687,7 +689,6 @@
             fields,
             fields,
             field,
-            pltpu.VMEM((2, ROWS + 2 * GUARD, 128), F32),
             pltpu.VMEM((9 * CHANNELS, CHANNELS), BF16),
             pltpu.VMEM((9 * CHANNELS, CHANNELS), BF16),
             pltpu.SMEM((2, 2), jnp.int32),

time: 62.3 us -> 61.3 us (0.984)
  Pallas kernels: 61.2 us -> 60.5 us
    pallas_call x1, Pallas kernels: 59.4 us -> 58.7 us  [window_grads(): pl.pallas_call(window_kernel, out_shape=[jax.ShapeDtypeStruct(early, BF16...]
where the time goes in v5:
time: 61.3 us; the launch traced here: 61.1 us
  Pallas kernels  60.5 us (99%)
  between operations  0.65 us (1%)
    pallas_call x1, Pallas kernels, window_grads(): pl.pallas_call(window_kernel, out_shape=[jax.ShapeDtypeStruct(early, BF16...  58.7 us
    pallas_call x1, Pallas kernels, updates(): pl.pallas_call(adam_kernel, out_shape=shapes * 4, in_specs=[pl.BlockSpec(...  1.79 us

profile of v5, /device:TPU:2, one launch (start us, length us, event | category | flops | bytes accessed | tf_op | source)
XLA Modules:
  0.0 61.1 jit_solution(2011065828495533933)
XLA Ops:
  0.6 58.7 %window.1 = (bf16[8,32,128]{2,1,0:T(8,128)(2,1)}, bf16[8,24,128]{2,1,0:T(8,128)(2,1)}) custom-call(s32[2,2]{1,0:T(2,128)} %moves_in.1, s32[2,2]{1,0:T(2,128)} %values_in.1, s32[2,2]{1,0:T(2,128)} %rewards_in.1, bf16[19,19,2,256]{3,2,1,0:T(2,128)(2,1)} %bitcast.1, f32[3,3,2,128]{3,2,1,0:T(2,128)} %refs_2_.1, f32[3,3,2,128]{3,2,1,0:T(2,128)} %refs_3_.1, ...), custom_call_target="tpu_custom_call" | custom-call | tf_op jit(solution)/shard_map/window/pallas_call | solution.py:657
  59.3 1.8 %adam.1 = (f32[3,3,2,128]{3,2,1,0:T(2,128)}, f32[3,3,2,128]{3,2,1,0:T(2,128)}, f32[1,2,601]{2,1,0:T(2,128)}, f32[1,2]{1,0:T(1,128)}, f32[3,3,2,128]{3,2,1,0:T(2,...) custom-call(bf16[8,32,128]{2,1,0:T(8,128)(2,1)} %get-tuple-element.3, ...), custom_call_target="tpu_custom_call" | custom-call | tf_op jit(solution)/shard_map/adam/pallas_call | solution.py:764

commit v6 on v5

--- a/solution.py
+++ b/solution.py
@@ -29,6 +29,7 @@
 )
 HALVES = (("dp_2", "dp_0"), ("dp_0", "dp_2"))
 ORDER = (1, 3, 2)
+FARTHEST = (4, 3, 5, 2, 6, 1, 7)
 SCALE = (9.0 * CHANNELS) ** (-0.5)
 
 head_scale = 4.0
@@ -121,7 +122,7 @@
         z = self.z
         for group in (1, 0):
             ref = self.stage.at[group, z]
-            for step in range(1, 8):
+            for step in FARTHEST:
                 peer = {"dp_1": lax.rem(z + step, 8)}
                 self.launch(remote(ref, ref, self.z_send.at[group, step], self.z_recv.at[group, z], peer))
 
@@ -294,7 +295,7 @@
         rows = letters.shape[1]
         for spot in range(8):
             letters[spot] = self.flat[pl.ds(16 * item + spot, rows, stride=8), :].astype(BF16)
-        for step in range(1, 8):
+        for step in FARTHEST:
             peer = lax.rem(self.z + step, 8)
             self.launch(
                 remote(

time: 61.3 us -> 60.7 us (level)
  no operation moved by 1% of the time
where the time goes in v6:
time: 60.7 us; the launch traced here: 60.5 us
  Pallas kernels  59.9 us (99%)
  between operations  0.65 us (1%)
    pallas_call x1, Pallas kernels, window_grads(): pl.pallas_call(window_kernel, out_shape=[jax.ShapeDtypeStruct(early, BF16...  58.1 us
    pallas_call x1, Pallas kernels, updates(): pl.pallas_call(adam_kernel, out_shape=shapes * 4, in_specs=[pl.BlockSpec(...  1.79 us

profile of v6, /device:TPU:2, one launch (start us, length us, event | category | flops | bytes accessed | tf_op | source)
XLA Modules:
  0.0 60.5 jit_solution(8870750200249851982)
XLA Ops:
  0.6 58.1 %window.1 = (bf16[8,32,128]{2,1,0:T(8,128)(2,1)}, bf16[8,24,128]{2,1,0:T(8,128)(2,1)}) custom-call(s32[2,2]{1,0:T(2,128)} %moves_in.1, s32[2,2]{1,0:T(2,128)} %values_in.1, s32[2,2]{1,0:T(2,128)} %rewards_in.1, bf16[19,19,2,256]{3,2,1,0:T(2,128)(2,1)} %bitcast.1, f32[3,3,2,128]{3,2,1,0:T(2,128)} %refs_2_.1, f32[3,3,2,128]{3,2,1,0:T(2,128)} %refs_3_.1, ...), custom_call_target="tpu_custom_call" | custom-call | tf_op jit(solution)/shard_map/window/pallas_call | solution.py:658
  58.7 1.8 %adam.1 = (f32[3,3,2,128]{3,2,1,0:T(2,128)}, f32[3,3,2,128]{3,2,1,0:T(2,128)}, f32[1,2,601]{2,1,0:T(2,128)}, f32[1,2]{1,0:T(1,128)}, f32[3,3,2,128]{3,2,1,0:T(2,...) custom-call(bf16[8,32,128]{2,1,0:T(8,128)(2,1)} %get-tuple-element.3, ...), custom_call_target="tpu_custom_call" | custom-call | tf_op jit(solution)/shard_map/adam/pallas_call | solution.py:765
